TPU v7x, 32 devices: a whole 2x2x4 slice. The times are simulated.
32 devices in a mesh: leaf: 8 (over z, y), blk: 4 (over x, core).
Axes of the slice: x: 2, y: 2, z: 4, core: 2. Of those that a mesh axis runs over, the one named last changes fastest.
Arguments:
- src_pos: int32 [4, 2097152], P('blk', 'leaf'), may hold values from 0 to 8388607, as said below
- strengths: float32 [2, 4, 2097152], P(None, 'blk', 'leaf'), may hold values from -0.001953125 to 0.001953125
- tgt_pos: int32 [8388608], P(('leaf', 'blk')), may hold values from 0 to 201326591, as said below
Outputs:
- field: float32 [2, 8388608], P(None, ('leaf', 'blk'))
Inputs may be any that keep to these rules, and one draw needn't show every extreme that they name: `src_pos`: row q holds 16384 runs of 128 cells; run b lies in the 128 cells from (q * 16384 + b) * 128 on. `tgt_pos`: the ticks held by index k of leaf, at every index of blk, come in 2048 runs of 128; run j lies in the 12288 ticks from (j * 8 + r) * 12288 on, where r is k with its 3 binary digits in reverse order.
All inputs are finite; a program needn't handle non-finite values.
Results may differ from a plain program's by a relative error of at most 0.0003.
Values sent between devices are 32-bit elements; how exact they have to be, the bound alone decides.
A program may use at most 128 MiB of HBM per device.

v0:
```python
import functools
import math

import jax
import jax.numpy as jnp
import numpy as np
from jax import lax
from jax.experimental import pallas as pl
from jax.experimental.pallas import tpu as pltpu
from jax.sharding import PartitionSpec as P

R = 16
PER_BOX = 128
TGT_BOX = 128
BOX_CELLS = 128
TOP_TICKS = 201326592
LANES = 128
HIGHEST = lax.Precision.HIGHEST


def fit_even(values, span, count):
    u = 0.5 * span * span * (1.0 + np.cos(np.pi * (np.arange(400) + 0.5) / 400))
    cheb = np.polynomial.chebyshev.Chebyshev.fit(u, values(np.sqrt(u)), count - 1, domain=[0, span * span])
    return [float(c) for c in cheb.convert(kind=np.polynomial.Polynomial).coef]


COS_POLY = fit_even(lambda y: np.cos(np.pi * y), 0.5, 5)
SIN_POLY = fit_even(lambda y: np.sin(np.pi * y) / y, 0.5, 4)


def horner(coefs, u):
    out = u * coefs[-1] + coefs[-2]
    for c in coefs[-3::-1]:
        out = out * u + c
    return out


def cos_sin_turns(y):
    u = y * y
    c, s = horner(COS_POLY, u), y * horner(SIN_POLY, u)
    twice = s + s
    return 1.0 - twice * s, twice * c


def node_offsets(box_cells):
    node_index = np.arange(R)
    unit_nodes = (1.0 - np.cos(np.pi * (node_index + 0.5) / R)) / 2.0
    return np.floor(box_cells * unit_nodes).astype(np.int64)


def lagrange_values(node_pos, points):
    rows = []
    for row_node in range(node_pos.shape[0]):
        column = np.ones(points.shape[0])
        for other in range(node_pos.shape[0]):
            if other != row_node:
                column = column * (points - node_pos[other]) / (node_pos[row_node] - node_pos[other])
        rows.append(column)
    return np.stack(rows)


def as_real(m):
    return np.block([[m.real, -m.imag], [m.imag, m.real]])


def turn64(a, b):
    product = (a * b + 2**31) % 2**32 - 2**31
    return product * (2.0 * np.pi / 2.0**32)


@functools.cache
def step_matrix(level):
    cells = BOX_CELLS * 2**level
    child, parent = node_offsets(cells), node_offsets(2 * cells)
    inner = np.concatenate([child, child + cells])
    blend = lagrange_values(parent / (2.0 * cells), inner / (2.0 * cells)).reshape(R, 2, R)
    half = TOP_TICKS // 2 ** (level + 2)
    assert half * cells % 2**32 == 2**31
    out = np.zeros((2, 2, 2 * R, 2 * R))
    for e in range(2):
        phase = np.exp(1j * turn64(half if e else -half, child))
        for j in range(2):
            out[e, j] = as_real((-1.0) ** j * blend[:, j, :] * phase[None, :])
    return out


def radix_matrix(first, count):
    total = np.eye(2 * R)[None, None]
    for k in range(count):
        m = step_matrix(first + k)
        n = total.shape[0]
        new = np.zeros((2 * n, 2 * n, 2 * R, 2 * R))
        for a in range(n):
            for b in range(n):
                for e in range(2):
                    for j in range(2):
                        new[2 * a + e, b + j * n] = m[e, j] @ total[a, b]
        total = new
    n = total.shape[0]
    return total.transpose(0, 2, 1, 3).reshape(n * 2 * R, n * 2 * R)


def fold_pairs():
    eye = np.eye(R)
    plus = eye[: R // 2] + eye[::-1][: R // 2]
    minus = eye[: R // 2] - eye[::-1][: R // 2]
    zero = np.zeros_like(plus)
    return np.block([[plus, zero], [zero, plus], [zero, -minus], [minus, zero]])


def leaf_matrix():
    nodes = node_offsets(BOX_CELLS)
    angles = np.pi * (np.arange(R) + 0.5) / R
    at_exact = lagrange_values(2.0 * nodes / BOX_CELLS - 1.0, np.cos(angles))
    cheb_at = np.stack([np.cos(n * angles) for n in range(R)])
    norm = np.where(np.arange(R) == 0, 1.0, 2.0) / R
    g = (norm[:, None] * (cheb_at @ at_exact.T)).astype(np.float32)
    wide = np.repeat(g.T, 8, axis=1)
    zero = np.zeros_like(wide)
    return np.block([[wide, zero], [zero, wide]]).astype(np.float32)


def leaf_kernel(pos_ref, str_ref, mix_ref, out_ref, p_t, re_t, im_t, *, digits):
    def turn_over(beta, slot):
        rows = pl.ds(beta, LANES, stride=digits)
        p_t[slot] = pos_ref[rows, :].T
        re_t[slot] = str_ref[0, rows, :].T
        im_t[slot] = str_ref[1, rows, :].T

    def tile(beta, carry):
        slot = lax.rem(beta, 2)
        turn_over(jnp.minimum(beta + 1, digits - 1), 1 - slot)
        zero = jnp.zeros((8, LANES), jnp.float32)
        acc = tuple((zero, zero) for _ in range(R))
        for i in range(PER_BOX // 8):
            acc = chunk(slot, i, acc)
        low, high = list(acc[: R // 2]), list(acc[R // 2 :])
        top = [high[0]]
        for k in range(1, R // 2):
            top.append(tuple(2.0 * h - m for h, m in zip(high[k], low[R // 2 - k])))
        both = low + top
        stack = jnp.concatenate([x for x, _ in both] + [y for _, y in both], axis=0)
        out_ref[beta] = jnp.dot(mix_ref[...], stack, precision=HIGHEST, preferred_element_type=jnp.float32)
        return carry

    def chunk(slot, i, acc):
        here = pl.ds(i * 8, 8)
        r = p_t[slot, here, :] & (BOX_CELLS - 1)
        turn = (r * (TOP_TICKS // 2)).astype(jnp.float32) * (2.0**-32)
        c, s = cos_sin_turns(turn)
        a, b = re_t[slot, here, :], im_t[slot, here, :]
        v = r.astype(jnp.float32) * (2.0 / BOX_CELLS) - 1.0
        v2 = v + v
        cheb = [None, v]
        for k in range(2, R // 2 + 1):
            cheb.append(v2 * v - 1.0 if k == 2 else v2 * cheb[-1] - cheb[-2])
        x, y = c * a - s * b, s * a + c * b
        out = []
        for part, (x, y) in enumerate([(x, y), (cheb[-1] * x, cheb[-1] * y)]):
            for k in range(R // 2):
                u, w = acc[part * (R // 2) + k]
                out.append((u + x, w + y) if k == 0 else (u + cheb[k] * x, w + cheb[k] * y))
        return tuple(out)

    turn_over(0, 0)
    lax.fori_loop(0, digits, tile, 0)


def leaf_call(pos, strengths):
    boxes = pos.shape[0]
    digits = boxes // LANES
    whole = pl.BlockSpec(memory_space=pltpu.VMEM)
    return pl.pallas_call(
        functools.partial(leaf_kernel, digits=digits),
        out_shape=jax.ShapeDtypeStruct((digits, 2 * R, LANES), jnp.float32),
        in_specs=[whole, whole, whole],
        out_specs=whole,
        scratch_shapes=[
            pltpu.VMEM((2, LANES, LANES), jnp.int32),
            pltpu.VMEM((2, LANES, LANES), jnp.float32),
            pltpu.VMEM((2, LANES, LANES), jnp.float32),
        ],
        name="leaf",
    )(pos, strengths, jnp.asarray(leaf_matrix()))


MAGIC = 1.5 * 2.0**23


def finish_kernel(w_ref, tgt_hbm, m_ref, out_hbm, tgt, out, bufs, got, coefs, g_t, re_t, im_t,
                  send, recv, gsend, grecv, tsem, osem, *, leaves, blocks, chunks, depth, rows):
    leaf_no, blk_no = lax.axis_index("leaf"), lax.axis_index("blk")
    bits = leaves.bit_length() - 1
    boxes = w_ref.shape[1]
    width = boxes // chunks
    tiles = width // LANES
    cells = BOX_CELLS * 2**depth
    ticks = TOP_TICKS // 2**depth
    half = R // 2
    sides = [leaf_no // 2**k % 2 for k in range(bits)]
    partners = [leaf_no + (1 - 2 * sides[k]) * 2**k for k in range(bits)]
    suffix = jnp.int32(0)
    for k in range(bits):
        suffix = 2 * suffix + sides[k]
    peers = [lax.rem(blk_no + d, blocks) for d in range(1, blocks)]
    fetch = pltpu.make_async_copy(tgt_hbm, tgt, tsem)
    fetch.start()

    barrier = pltpu.get_barrier_semaphore()
    for k in range(bits):
        pl.semaphore_signal(barrier, inc=1, device_id=(partners[k], blk_no), device_id_type=pl.DeviceIdType.MESH)
    for peer in peers:
        pl.semaphore_signal(barrier, inc=1, device_id=(leaf_no, peer), device_id_type=pl.DeviceIdType.MESH)
    pl.semaphore_wait(barrier, bits + blocks - 1)

    def own(stage, c):
        return w_ref.at[:, pl.ds(c * width, width)] if stage == 0 else bufs.at[stage - 1, c]

    def exchange(stage, c):
        return pltpu.make_async_remote_copy(
            src_ref=own(stage, c), dst_ref=got.at[stage, c],
            send_sem=send.at[stage, c], recv_sem=recv.at[stage, c],
            device_id=(partners[stage], blk_no), device_id_type=pl.DeviceIdType.MESH,
        )

    def spread(d, c):
        here = coefs.at[blk_no, pl.ds(c * tiles, tiles)]
        return pltpu.make_async_remote_copy(
            src_ref=here, dst_ref=here,
            send_sem=gsend.at[d - 1, c], recv_sem=grecv.at[d - 1, c],
            device_id=(leaf_no, peers[d - 1]), device_id_type=pl.DeviceIdType.MESH,
        )

    def combine(todo):
        for stage, c in todo:
            exchange(stage, c).wait_recv()
        results = []
        for stage, c in todo:
            pair = jnp.concatenate([own(stage, c)[...], got[stage, c]], axis=0)
            results.append(mm(m_ref[stage, sides[stage]], pair))
        for (stage, c), w in zip(todo, results):
            if stage < bits - 1:
                bufs[stage, c] = w
            else:
                for i in range(tiles):
                    coefs[blk_no, c * tiles + i] = w[:, i * LANES : (i + 1) * LANES]
        for stage, c in todo:
            if stage < bits - 1:
                exchange(stage + 1, c).start()
            else:
                for d in range(1, blocks):
                    spread(d, c).start()

    offsets = 2 * node_offsets(cells) - cells + 1

    def turned(g, factor):
        y = g * factor
        if abs(factor) * (ticks // 2) > 0.5:
            y = y - ((y + MAGIC) - MAGIC)
        return cos_sin_turns(y)

    lane = lax.broadcasted_iota(jnp.int32, (1, LANES), 1)

    def evaluate(tile, carry):
        box = (tile * LANES + lane) * leaves + suffix
        center = box * ticks + ticks // 2
        first = pl.multiple_of(tile * LANES, LANES)
        g_t[...] = (tgt[pl.ds(first, LANES), :].T - center).astype(jnp.float32)

        def chunk(i, carry):
            here = pl.ds(pl.multiple_of(i * rows, rows), rows)
            g = g_t[here, :]
            acc = [[None, None] for _ in range(blocks)]
            for t in range(half):
                c, s = turned(g, float(offsets[t]) * 2.0**-33)
                for q in range(blocks):
                    for part in range(2):
                        sc = coefs[q, tile, pl.ds(part * half + t, 1), :]
                        sd = coefs[q, tile, pl.ds((2 + part) * half + t, 1), :]
                        term = sc * c + sd * s
                        acc[q][part] = term if t == 0 else acc[q][part] + term
            zc, zs = turned(g, float(cells) * 2.0**-32)
            re, im = acc[blocks - 1]
            for q in range(blocks - 2, -1, -1):
                re, im = zc * re - zs * im + acc[q][0], zc * im + zs * re + acc[q][1]
            pc, ps = turned(g, float(cells - 1) * 2.0**-33)
            re_t[here, :] = pc * re - ps * im
            im_t[here, :] = pc * im + ps * re
            return carry

        lax.fori_loop(0, TGT_BOX // rows, chunk, 0)
        out[pl.ds(2 * first, LANES, stride=2), :] = re_t[...].T
        out[pl.ds(2 * first + 1, LANES, stride=2), :] = im_t[...].T
        return carry

    def put(c):
        span = pl.ds(2 * c * width, 2 * width)
        return pltpu.make_async_copy(out.at[span], out_hbm.at[span], osem.at[c])

    def field(c):
        if c == 0:
            fetch.wait()
        for d in range(1, blocks):
            spread(d, c).wait_recv()
        lax.fori_loop(c * tiles, (c + 1) * tiles, evaluate, 0)
        put(c).start()

    ahead = min(3, chunks)
    for c in range(ahead):
        exchange(0, c).start()
    for step in range(chunks + bits):
        combine([(k, step - k) for k in range(bits - 1, -1, -1) if 0 <= step - k < chunks])
        if step + ahead < chunks:
            exchange(0, step + ahead).start()
        if step >= bits:
            field(step - bits)
    for c in range(chunks):
        for stage in range(bits):
            exchange(stage, c).wait_send()
        for d in range(1, blocks):
            spread(d, c).wait_send()
        put(c).wait()


def finish_call(weights, ticks, matrices, leaves, blocks, depth, chunks):
    boxes = ticks.shape[0]
    bits = leaves.bit_length() - 1
    width = boxes // chunks
    whole = pl.BlockSpec(memory_space=pltpu.VMEM)
    anywhere = pl.BlockSpec(memory_space=pl.ANY)
    dma = pltpu.SemaphoreType.DMA
    return pl.pallas_call(
        functools.partial(finish_kernel, leaves=leaves, blocks=blocks, chunks=chunks, depth=depth, rows=16),
        out_shape=jax.ShapeDtypeStruct((2 * boxes, TGT_BOX), jnp.float32),
        in_specs=[whole, anywhere, whole],
        out_specs=anywhere,
        scratch_shapes=[
            pltpu.VMEM((boxes, TGT_BOX), jnp.int32),
            pltpu.VMEM((2 * boxes, TGT_BOX), jnp.float32),
            pltpu.VMEM((bits - 1, chunks, 2 * R, width), jnp.float32),
            pltpu.VMEM((bits, chunks, 2 * R, width), jnp.float32),
            pltpu.VMEM((blocks, boxes // LANES, 2 * R, LANES), jnp.float32),
        ] + [pltpu.VMEM((TGT_BOX, LANES), jnp.float32)] * 3 + [
            dma((bits, chunks)), dma((bits, chunks)),
            dma((blocks - 1, chunks)), dma((blocks - 1, chunks)),
            dma, dma((chunks,)),
        ],
        compiler_params=pltpu.CompilerParams(collective_id=0, has_side_effects=True),
        name="finish",
    )(weights, ticks, matrices)


def table(m):
    return jnp.asarray(m.astype(np.float32))


def mm(a, b):
    return jnp.dot(a, b, precision=HIGHEST, preferred_element_type=jnp.float32)


def local_tree(leaf, boxes):
    low = leaf.shape[0]
    n1 = low.bit_length() - 1
    rest = boxes.bit_length() - 1 - n1
    n2 = rest - rest // 2
    n3 = rest - n2
    c = 2 * R
    y = mm(table(radix_matrix(0, n1)), leaf.reshape(low * c, -1))
    y = y.reshape(low, c, 2**n3, 2**n2).transpose(3, 1, 0, 2).reshape(2**n2 * c, -1)
    y = mm(table(radix_matrix(n1, n2)), y)
    y = y.reshape(2**n2, c, low, 2**n3).transpose(3, 1, 2, 0).reshape(2**n3 * c, -1)
    y = mm(table(radix_matrix(n1 + n2, n3)), y)
    return y.reshape(2**n3, c, low * 2**n2).transpose(1, 2, 0).reshape(c, boxes)


def local(src_pos, strengths, tgt_pos):
    leaf_count = lax.axis_size("leaf")
    leaf_bits = leaf_count.bit_length() - 1
    boxes = src_pos.shape[1] // PER_BOX
    local_depth = boxes.bit_length() - 1
    leaf = leaf_call(src_pos.reshape(boxes, PER_BOX), strengths.reshape(2, boxes, PER_BOX))
    weights = local_tree(leaf, boxes)
    steps = np.stack([step_matrix(local_depth + k) for k in range(leaf_bits)])
    steps[-1] = np.einsum("xy,ejyz->ejxz", fold_pairs(), steps[-1])
    steps[:, 1] = steps[:, 1, ::-1]
    steps = np.concatenate([steps[:, :, 0], steps[:, :, 1]], axis=-1)
    out = finish_call(
        weights, tgt_pos.reshape(boxes, TGT_BOX), table(steps), leaf_count, lax.axis_size("blk"),
        local_depth + leaf_bits, 8,
    )
    return out.reshape(boxes, 2, TGT_BOX).transpose(1, 0, 2).reshape(2, boxes * TGT_BOX)


def solution(mesh):
    return jax.shard_map(
        local,
        mesh=mesh,
        in_specs=(P("blk", "leaf"), P(None, "blk", "leaf"), P(("leaf", "blk"))),
        out_specs=P(None, ("leaf", "blk")),
        check_vma=False,
    )
```

profile of v0, /device:TPU:0, one launch (start us, length us, event | category | flops | bytes accessed | tf_op | source)
XLA Modules:
  0.0 72.2 jit_solution(17958447787370234072)
XLA Ops:
  0.0 0.0 copy-start.1
  0.0 12.1 %leaf.1 = f32[16,32,128]{2,1,0:T(8,128)} custom-call(s32[2048,128]{1,0:T(8,128)} %bitcast.39, f32[2,2048,128]{2,1,0:T(8,128)} %bitcast.37, f32[32,256]{1,0:T(8,128)} %constant.10.clone.mix_ref), custom_call_target="tpu_custom_call" | custom-call | tf_op jit(solution)/shard_map/leaf/pallas_call | solution.py:173
  12.1 0.0 copy-done.1
  12.1 2.1 %fusion = f32[512,128]{0,1:T(8,128)S(1)} fusion(f32[512,512]{1,0:T(8,128)S(1)} %copy-done.1, f32[512,128]{1,0:T(8,128)} %bitcast.41), kind=kOutput, calls=%fused_computation | convolution fusion | flops 402653184 | bytes 1572864 | tf_op jit(solution)/shard_map/dot_general | solution.py:358
  14.2 0.0 copy-start
  14.3 0.3 reshape.39
  14.5 0.3 copy.12
  14.9 0.4 reshape.40
  15.3 0.2 copy-done
  15.5 1.2 %fusion.1 = f32[512,128]{0,1:T(8,128)S(1)} fusion(f32[512,512]{1,0:T(8,128)S(1)} %copy-done, f32[512,128]{0,1:T(8,128)S(1)} %reshape.40), kind=kOutput, calls=%fused_computation.1 | convolution fusion | flops 402653184 | bytes 1572864 | tf_op jit(solution)/shard_map/dot_general | solution.py:358
  16.7 0.0 copy-start.2
  16.7 0.3 reshape.41
  17.0 0.3 copy.14
  17.3 0.3 reshape.42
  17.6 0.0 copy-done.2
  17.6 0.4 fusion.2
  18.1 0.4 copy.15
  18.5 1.0 %copy.16.w_ref = f32[32,2048]{1,0:T(8,128)} copy(f32[32,2048]{0,1:T(8,128)S(1)} %bitcast.34) | data formatting | bytes 524288 | tf_op jit(solution)/shard_map/reshape | solution.py:373
  19.5 50.0 %finish.1 = f32[4096,128]{1,0:T(8,128)} custom-call(f32[32,2048]{1,0:T(8,128)} %copy.16.w_ref, s32[2048,128]{1,0:T(8,128)} %bitcast.40, f32[3,2,32,64]{3,2,1,0:T(8,128)} %constant.14.clone.m_ref), custom_call_target="tpu_custom_call" | custom-call | tf_op jit(solution)/shard_map/finish/pallas_call | solution.py:332
  69.5 2.6 %copy.21 = f32[2,262144]{1,0:T(2,128)} copy(f32[2,262144]{1,0:T(2,128)} %bitcast.33) | data formatting | bytes 4194304
Async XLA Ops:
  0.0 12.1 %copy-start.1 = (f32[512,512]{1,0:T(8,128)S(1)}, f32[512,512]{1,0:T(8,128)}, u32[]{:S(2)}) copy-start(f32[512,512]{1,0:T(8,128)} %constant.11.clone) | copy-start | bytes 3145732
  14.2 1.2 %copy-start = (f32[512,512]{1,0:T(8,128)S(1)}, f32[512,512]{1,0:T(8,128)}, u32[]{:S(2)}) copy-start(f32[512,512]{1,0:T(8,128)} %constant.12.clone) | copy-start | bytes 3145732
  16.7 1.0 %copy-start.2 = (f32[256,256]{1,0:T(8,128)S(1)}, f32[256,256]{1,0:T(8,128)}, u32[]{:S(2)}) copy-start(f32[256,256]{1,0:T(8,128)} %constant.13.clone) | copy-start | bytes 786436
where the time goes:
time: 72.4 us; the launch traced here: 72.2 us
  Pallas kernels  62.1 us (86%)
  local copies, waits for them, and re-layouts  6.18 us (9%)
  matrix products  3.76 us (5%)
    pallas_call x1, Pallas kernels, finish_call(): pl.pallas_call(functools.partial(finish_kernel, leaves=leaves, blocks=blo...  50 us
    pallas_call x1, Pallas kernels, leaf_call(): pl.pallas_call(functools.partial(leaf_kernel, digits=digits), out_shape=j...  12.1 us
    dot_general x3, matrix products, mm(): return jnp.dot(a, b, precision=HIGHEST, preferred_element_type=jnp.float32)  3.76 us
    unnamed x7, local copies, waits for them, and re-layouts  2.79 us

commit v1 on v0

--- a/solution.py
+++ b/solution.py
@@ -100,12 +100,42 @@
     return total.transpose(0, 2, 1, 3).reshape(n * 2 * R, n * 2 * R)
 
 
-def fold_pairs():
-    eye = np.eye(R)
-    plus = eye[: R // 2] + eye[::-1][: R // 2]
-    minus = eye[: R // 2] - eye[::-1][: R // 2]
-    zero = np.zeros_like(plus)
-    return np.block([[plus, zero], [zero, plus], [zero, -minus], [minus, zero]])
+DEGREE = 4
+
+
+def fit_turn(theta):
+    s = np.cos(np.pi * (np.arange(64) + 0.5) / 64)
+    fit = np.polynomial.chebyshev.chebfit(s, np.exp(1j * s[:, None] * theta[None, :]), DEGREE)
+    power = np.zeros((DEGREE + 1, DEGREE + 1))
+    for n in range(DEGREE + 1):
+        c = np.polynomial.chebyshev.cheb2poly(np.eye(DEGREE + 1)[n])
+        power[: len(c), n] = c
+    return power @ fit
+
+
+@functools.cache
+def grid_matrix(depth, blocks):
+    cells = BOX_CELLS * 2**depth
+    ticks = TOP_TICKS // 2**depth
+    step = ticks // LANES
+    assert step * LANES == ticks and step % 2 == 0
+    nodes = (np.arange(blocks)[:, None] * cells + node_offsets(cells)[None, :]).reshape(-1)
+    centers = np.arange(LANES) * step + step // 2 - ticks // 2
+    phase = np.exp(1j * turn64(centers[None, :], nodes[:, None]))
+    off = (nodes - (blocks * cells - 1) / 2.0) * (step // 2) * (2.0 * np.pi / 2.0**32)
+    poly = fit_turn(off)
+    out = np.zeros((blocks, 2, R, DEGREE + 1, 2, LANES))
+    for p in range(DEGREE + 1):
+        b = (poly[p][:, None] * phase).reshape(blocks, R, LANES)
+        out[:, 0, :, p, 0], out[:, 0, :, p, 1] = b.real, b.imag
+        out[:, 1, :, p, 0], out[:, 1, :, p, 1] = -b.imag, b.real
+    return out.reshape(blocks * 2 * R, (DEGREE + 1) * 2 * LANES)
+
+
+def split_rows(m):
+    hi = m.astype(jnp.bfloat16)
+    lo = (m - hi.astype(np.float64)).astype(jnp.bfloat16)
+    return jnp.asarray(np.concatenate([hi, hi, lo], axis=0))
 
 
 def leaf_matrix():
@@ -184,11 +214,8 @@
     )(pos, strengths, jnp.asarray(leaf_matrix()))
 
 
-MAGIC = 1.5 * 2.0**23
-
-
-def finish_kernel(w_ref, tgt_hbm, m_ref, out_hbm, tgt, out, bufs, got, coefs, g_t, re_t, im_t,
-                  send, recv, gsend, grecv, tsem, osem, *, leaves, blocks, chunks, depth, rows):
+def finish_kernel(w_ref, tgt_hbm, m_ref, a_hbm, out_hbm, tgt, out, a_buf, tab, bufs, got, coefs,
+                  send, recv, gsend, grecv, tsem, asem, osem, *, leaves, blocks, chunks, depth, rows):
     leaf_no, blk_no = lax.axis_index("leaf"), lax.axis_index("blk")
     bits = leaves.bit_length() - 1
     boxes = w_ref.shape[1]
@@ -196,7 +223,6 @@
     tiles = width // LANES
     cells = BOX_CELLS * 2**depth
     ticks = TOP_TICKS // 2**depth
-    half = R // 2
     sides = [leaf_no // 2**k % 2 for k in range(bits)]
     partners = [leaf_no + (1 - 2 * sides[k]) * 2**k for k in range(bits)]
     suffix = jnp.int32(0)
@@ -205,6 +231,8 @@
     peers = [lax.rem(blk_no + d, blocks) for d in range(1, blocks)]
     fetch = pltpu.make_async_copy(tgt_hbm, tgt, tsem)
     fetch.start()
+    load = pltpu.make_async_copy(a_hbm, a_buf, asem)
+    load.start()
 
     barrier = pltpu.get_barrier_semaphore()
     for k in range(bits):
@@ -251,46 +279,36 @@
                 for d in range(1, blocks):
                     spread(d, c).start()
 
-    offsets = 2 * node_offsets(cells) - cells + 1
-
-    def turned(g, factor):
-        y = g * factor
-        if abs(factor) * (ticks // 2) > 0.5:
-            y = y - ((y + MAGIC) - MAGIC)
-        return cos_sin_turns(y)
-
-    lane = lax.broadcasted_iota(jnp.int32, (1, LANES), 1)
+    pitch = ticks // LANES
+    tilt = (blocks * cells - 1) / 2.0 * (pitch // 2) / 2.0**32
+    cos_poly = fit_even(lambda y: np.cos(2 * np.pi * y), tilt, 3)
+    sin_poly = fit_even(lambda y: np.sin(2 * np.pi * y) / y, tilt, 3)
+    cos_poly = [c * tilt ** (2 * k) for k, c in enumerate(cos_poly)]
+    sin_poly = [c * tilt ** (2 * k + 1) for k, c in enumerate(sin_poly)]
+    below = lax.broadcasted_iota(jnp.int32, (rows, LANES), 0) * (leaves * ticks)
 
     def evaluate(tile, carry):
-        box = (tile * LANES + lane) * leaves + suffix
-        center = box * ticks + ticks // 2
+        whole = jnp.concatenate([coefs[q, tile] for q in range(blocks)], axis=0).T
+        hi = whole.astype(jnp.bfloat16)
+        lo = (whole - hi.astype(jnp.float32)).astype(jnp.bfloat16)
+        lhs = jnp.concatenate([hi, lo, hi], axis=1)
+        for n in range(2 * (DEGREE + 1)):
+            tab[n] = jnp.dot(lhs, a_buf[:, n * LANES : (n + 1) * LANES], preferred_element_type=jnp.float32)
         first = pl.multiple_of(tile * LANES, LANES)
-        g_t[...] = (tgt[pl.ds(first, LANES), :].T - center).astype(jnp.float32)
-
-        def chunk(i, carry):
-            here = pl.ds(pl.multiple_of(i * rows, rows), rows)
-            g = g_t[here, :]
-            acc = [[None, None] for _ in range(blocks)]
-            for t in range(half):
-                c, s = turned(g, float(offsets[t]) * 2.0**-33)
-                for q in range(blocks):
-                    for part in range(2):
-                        sc = coefs[q, tile, pl.ds(part * half + t, 1), :]
-                        sd = coefs[q, tile, pl.ds((2 + part) * half + t, 1), :]
-                        term = sc * c + sd * s
-                        acc[q][part] = term if t == 0 else acc[q][part] + term
-            zc, zs = turned(g, float(cells) * 2.0**-32)
-            re, im = acc[blocks - 1]
-            for q in range(blocks - 2, -1, -1):
-                re, im = zc * re - zs * im + acc[q][0], zc * im + zs * re + acc[q][1]
-            pc, ps = turned(g, float(cells - 1) * 2.0**-33)
-            re_t[here, :] = pc * re - ps * im
-            im_t[here, :] = pc * im + ps * re
-            return carry
-
-        lax.fori_loop(0, TGT_BOX // rows, chunk, 0)
-        out[pl.ds(2 * first, LANES, stride=2), :] = re_t[...].T
-        out[pl.ds(2 * first + 1, LANES, stride=2), :] = im_t[...].T
+        for i in range(LANES // rows):
+            base = ((first + i * rows) * leaves + suffix) * ticks
+            u = (tgt[pl.ds(first + i * rows, rows), :] - (below + base)).astype(jnp.float32)
+            cell = (u * (1.0 / pitch) + (0.5 / pitch)).astype(jnp.int32)
+            s = (u - cell.astype(jnp.float32) * pitch) * (2.0 / pitch) - 1.0
+            got_at = [jnp.take_along_axis(tab[n, i * rows : (i + 1) * rows, :], cell, axis=1)
+                      for n in range(2 * (DEGREE + 1))]
+            re, im = got_at[-2], got_at[-1]
+            for p in range(DEGREE - 1, -1, -1):
+                re, im = re * s + got_at[2 * p], im * s + got_at[2 * p + 1]
+            z = s * s
+            pc, ps = horner(cos_poly, z), s * horner(sin_poly, z)
+            out[pl.ds(2 * (first + i * rows), rows, stride=2), :] = pc * re - ps * im
+            out[pl.ds(2 * (first + i * rows) + 1, rows, stride=2), :] = pc * im + ps * re
         return carry
 
     def put(c):
@@ -300,6 +318,7 @@
     def field(c):
         if c == 0:
             fetch.wait()
+            load.wait()
         for d in range(1, blocks):
             spread(d, c).wait_recv()
         lax.fori_loop(c * tiles, (c + 1) * tiles, evaluate, 0)
@@ -322,7 +341,7 @@
         put(c).wait()
 
 
-def finish_call(weights, ticks, matrices, leaves, blocks, depth, chunks):
+def finish_call(weights, ticks, matrices, grid, leaves, blocks, depth, chunks):
     boxes = ticks.shape[0]
     bits = leaves.bit_length() - 1
     width = boxes // chunks
@@ -330,24 +349,26 @@
     anywhere = pl.BlockSpec(memory_space=pl.ANY)
     dma = pltpu.SemaphoreType.DMA
     return pl.pallas_call(
-        functools.partial(finish_kernel, leaves=leaves, blocks=blocks, chunks=chunks, depth=depth, rows=16),
+        functools.partial(finish_kernel, leaves=leaves, blocks=blocks, chunks=chunks, depth=depth, rows=8),
         out_shape=jax.ShapeDtypeStruct((2 * boxes, TGT_BOX), jnp.float32),
-        in_specs=[whole, anywhere, whole],
+        in_specs=[whole, anywhere, whole, anywhere],
         out_specs=anywhere,
         scratch_shapes=[
             pltpu.VMEM((boxes, TGT_BOX), jnp.int32),
             pltpu.VMEM((2 * boxes, TGT_BOX), jnp.float32),
+            pltpu.VMEM(grid.shape, jnp.bfloat16),
+            pltpu.VMEM((2 * (DEGREE + 1), LANES, LANES), jnp.float32),
             pltpu.VMEM((bits - 1, chunks, 2 * R, width), jnp.float32),
             pltpu.VMEM((bits, chunks, 2 * R, width), jnp.float32),
             pltpu.VMEM((blocks, boxes // LANES, 2 * R, LANES), jnp.float32),
-        ] + [pltpu.VMEM((TGT_BOX, LANES), jnp.float32)] * 3 + [
+        ] + [
             dma((bits, chunks)), dma((bits, chunks)),
             dma((blocks - 1, chunks)), dma((blocks - 1, chunks)),
-            dma, dma((chunks,)),
+            dma, dma, dma((chunks,)),
         ],
         compiler_params=pltpu.CompilerParams(collective_id=0, has_side_effects=True),
         name="finish",
-    )(weights, ticks, matrices)
+    )(weights, ticks, matrices, grid)
 
 
 def table(m):
@@ -381,11 +402,11 @@
     leaf = leaf_call(src_pos.reshape(boxes, PER_BOX), strengths.reshape(2, boxes, PER_BOX))
     weights = local_tree(leaf, boxes)
     steps = np.stack([step_matrix(local_depth + k) for k in range(leaf_bits)])
-    steps[-1] = np.einsum("xy,ejyz->ejxz", fold_pairs(), steps[-1])
     steps[:, 1] = steps[:, 1, ::-1]
     steps = np.concatenate([steps[:, :, 0], steps[:, :, 1]], axis=-1)
     out = finish_call(
-        weights, tgt_pos.reshape(boxes, TGT_BOX), table(steps), leaf_count, lax.axis_size("blk"),
+        weights, tgt_pos.reshape(boxes, TGT_BOX), table(steps),
+        split_rows(grid_matrix(local_depth + leaf_bits, lax.axis_size("blk"))), leaf_count, lax.axis_size("blk"),
         local_depth + leaf_bits, 8,
     )
     return out.reshape(boxes, 2, TGT_BOX).transpose(1, 0, 2).reshape(2, boxes * TGT_BOX)

time: 72.4 us -> 71 us (0.981)
  Pallas kernels: 62.1 us -> 60.7 us
    pallas_call x1, Pallas kernels: 50 us -> 48.6 us  [finish_call(): pl.pallas_call(functools.partial(finish_kernel, leaves=leaves, blocks=blo...]
where the time goes in v1:
time: 71 us; the launch traced here: 70.8 us
  Pallas kernels  60.7 us (85%)
  local copies, waits for them, and re-layouts  6.18 us (9%)
  matrix products  3.76 us (5%)
    pallas_call x1, Pallas kernels, finish_call(): pl.pallas_call(functools.partial(finish_kernel, leaves=leaves, blocks=blo...  48.6 us
    pallas_call x1, Pallas kernels, leaf_call(): pl.pallas_call(functools.partial(leaf_kernel, digits=digits), out_shape=j...  12.1 us
    dot_general x3, matrix products, mm(): return jnp.dot(a, b, precision=HIGHEST, preferred_element_type=jnp.float32)  3.76 us
    unnamed x7, local copies, waits for them, and re-layouts  2.79 us
    reshape x2, local copies, waits for them, and re-layouts, local_tree(): y.reshape(2 ** n3, c, low * 2 ** n2).transpose(1, 2, 0).reshape(c, boxes)  1.43 us

profile of v1, /device:TPU:0, one launch (start us, length us, event | category | flops | bytes accessed | tf_op | source)
XLA Modules:
  0.0 70.8 jit_solution(15867911115365882749)
XLA Ops:
  0.0 0.0 copy-start.1
  0.0 12.1 %leaf.1 = f32[16,32,128]{2,1,0:T(8,128)} custom-call(s32[2048,128]{1,0:T(8,128)} %bitcast.40, f32[2,2048,128]{2,1,0:T(8,128)} %bitcast.37, f32[32,256]{1,0:T(8,128)} %constant.12.clone.mix_ref), custom_call_target="tpu_custom_call" | custom-call | tf_op jit(solution)/shard_map/leaf/pallas_call | solution.py:203
  12.1 0.0 copy-done.1
  12.1 2.1 %fusion = f32[512,128]{0,1:T(8,128)S(1)} fusion(f32[512,512]{1,0:T(8,128)S(1)} %copy-done.1, f32[512,128]{1,0:T(8,128)} %bitcast.41), kind=kOutput, calls=%fused_computation | convolution fusion | flops 402653184 | bytes 1572864 | tf_op jit(solution)/shard_map/dot_general | solution.py:379
  14.2 0.0 copy-start
  14.3 0.3 reshape.39
  14.5 0.3 copy.13
  14.9 0.4 reshape.40
  15.3 0.2 copy-done
  15.5 1.2 %fusion.1 = f32[512,128]{0,1:T(8,128)S(1)} fusion(f32[512,512]{1,0:T(8,128)S(1)} %copy-done, f32[512,128]{0,1:T(8,128)S(1)} %reshape.40), kind=kOutput, calls=%fused_computation.1 | convolution fusion | flops 402653184 | bytes 1572864 | tf_op jit(solution)/shard_map/dot_general | solution.py:379
  16.7 0.0 copy-start.2
  16.7 0.3 reshape.41
  17.0 0.3 copy.15
  17.3 0.3 reshape.42
  17.6 0.0 copy-done.2
  17.6 0.4 fusion.2
  18.1 0.4 copy.16
  18.5 1.0 %copy.17.w_ref = f32[32,2048]{1,0:T(8,128)} copy(f32[32,2048]{0,1:T(8,128)S(1)} %bitcast.34) | data formatting | bytes 524288 | tf_op jit(solution)/shard_map/reshape | solution.py:394
  19.5 48.6 %finish.1 = f32[4096,128]{1,0:T(8,128)} custom-call(f32[32,2048]{1,0:T(8,128)} %copy.17.w_ref, s32[2048,128]{1,0:T(8,128)} %bitcast.38, f32[3,2,32,64]{3,2,1,0:T(8,128)} %constant.16.clone.m_ref, bf16[384,1280]{1,0:T(8,128)(2,1)} %constant.17.clone.a_hbm), custom_call_target="tpu_custom_call" | custom-call | tf_op jit(solution)/shard_map/finish/pallas_call | solution.py:351
  68.1 2.6 %copy.22 = f32[2,262144]{1,0:T(2,128)} copy(f32[2,262144]{1,0:T(2,128)} %bitcast.33) | data formatting | bytes 4194304
Async XLA Ops:
  0.0 12.1 %copy-start.1 = (f32[512,512]{1,0:T(8,128)S(1)}, f32[512,512]{1,0:T(8,128)}, u32[]{:S(2)}) copy-start(f32[512,512]{1,0:T(8,128)} %constant.13.clone) | copy-start | bytes 3145732
  14.2 1.2 %copy-start = (f32[512,512]{1,0:T(8,128)S(1)}, f32[512,512]{1,0:T(8,128)}, u32[]{:S(2)}) copy-start(f32[512,512]{1,0:T(8,128)} %constant.14.clone) | copy-start | bytes 3145732
  16.7 1.0 %copy-start.2 = (f32[256,256]{1,0:T(8,128)S(1)}, f32[256,256]{1,0:T(8,128)}, u32[]{:S(2)}) copy-start(f32[256,256]{1,0:T(8,128)} %constant.15.clone) | copy-start | bytes 786436

commit v2 on v1

--- a/solution.py
+++ b/solution.py
@@ -394,7 +394,7 @@
     return y.reshape(2**n3, c, low * 2**n2).transpose(1, 2, 0).reshape(c, boxes)
 
 
-def local(src_pos, strengths, tgt_pos):
+def local_butterfly(src_pos, strengths, tgt_pos):
     leaf_count = lax.axis_size("leaf")
     leaf_bits = leaf_count.bit_length() - 1
     boxes = src_pos.shape[1] // PER_BOX
@@ -412,7 +412,265 @@
     return out.reshape(boxes, 2, TGT_BOX).transpose(1, 0, 2).reshape(2, boxes * TGT_BOX)
 
 
+def xor(a, d, bits):
+    return sum(((a // 2**k % 2 + (d >> k) % 2) % 2) * 2**k for k in range(bits))
+
+
+def reverse_bits(a, bits):
+    return sum((a // 2**k % 2) * 2 ** (bits - 1 - k) for k in range(bits))
+
+
+def split_pair(x):
+    hi = x.astype(jnp.bfloat16)
+    return hi, (x - hi.astype(jnp.float32)).astype(jnp.bfloat16)
+
+
+def dot16(a, b):
+    return jnp.dot(a, b, preferred_element_type=jnp.float32)
+
+
+def far_first(leaves):
+    half = leaves // 2
+    return [1] + list(range(half, leaves)) + list(range(2, half)) if leaves > 2 else [1]
+
+
+def up_kernel(pos_ref, str_ref, mix_ref, w_hbm, out_ref, p_t, re_t, im_t, stack, w_buf, y, got,
+              send, recv, wsem, *, digits, leaves):
+    me, blk_no = lax.axis_index("leaf"), lax.axis_index("blk")
+    bits = leaves.bit_length() - 1
+    load = pltpu.make_async_copy(w_hbm, w_buf, wsem)
+    load.start()
+    barrier = pltpu.get_barrier_semaphore()
+    for d in range(1, leaves):
+        pl.semaphore_signal(barrier, inc=1, device_id=(xor(me, d, bits), blk_no), device_id_type=pl.DeviceIdType.MESH)
+    leaf_kernel(pos_ref, str_ref, mix_ref, stack, p_t, re_t, im_t, digits=digits)
+    hi, lo = split_pair(stack[...].reshape(digits * 2 * R, LANES))
+    load.wait()
+    y[...] = (dot16(w_buf[0], hi) + dot16(w_buf[0], lo) + dot16(w_buf[1], hi)).reshape(y.shape)
+    pl.semaphore_wait(barrier, leaves - 1)
+
+    def ship(d):
+        peer = xor(me, d, bits)
+        return pltpu.make_async_remote_copy(
+            src_ref=y.at[peer], dst_ref=got.at[me],
+            send_sem=send.at[d - 1], recv_sem=recv.at[d - 1],
+            device_id=(peer, blk_no), device_id_type=pl.DeviceIdType.MESH,
+        )
+
+    for d in far_first(leaves):
+        ship(d).start()
+    out_ref[me] = y[me]
+    for d in far_first(leaves):
+        ship(d).wait_recv()
+        peer = xor(me, d, bits)
+        out_ref[peer] = got[peer]
+    for d in far_first(leaves):
+        ship(d).wait_send()
+
+
+def up_call(pos, strengths, leaves):
+    boxes = pos.shape[0]
+    digits = boxes // LANES
+    whole = pl.BlockSpec(memory_space=pltpu.VMEM)
+    anywhere = pl.BlockSpec(memory_space=pl.ANY)
+    dma = pltpu.SemaphoreType.DMA
+    n = digits * 2 * R
+    part = (leaves, n // leaves, LANES)
+    return pl.pallas_call(
+        functools.partial(up_kernel, digits=digits, leaves=leaves),
+        out_shape=jax.ShapeDtypeStruct(part, jnp.float32),
+        in_specs=[whole, whole, whole, anywhere],
+        out_specs=whole,
+        scratch_shapes=[
+            pltpu.VMEM((2, LANES, LANES), jnp.int32),
+            pltpu.VMEM((2, LANES, LANES), jnp.float32),
+            pltpu.VMEM((2, LANES, LANES), jnp.float32),
+            pltpu.VMEM((digits, 2 * R, LANES), jnp.float32),
+            pltpu.VMEM((2, n, n), jnp.bfloat16),
+            pltpu.VMEM(part, jnp.float32),
+            pltpu.VMEM(part, jnp.float32),
+            dma((leaves - 1,)), dma((leaves - 1,)), dma,
+        ],
+        compiler_params=pltpu.CompilerParams(collective_id=0, has_side_effects=True),
+        name="up",
+    )(pos, strengths, jnp.asarray(leaf_matrix()), two_parts(radix_matrix(0, digits.bit_length() - 1)))
+
+
+def two_parts(m):
+    hi = m.astype(jnp.bfloat16)
+    return jnp.asarray(np.stack([hi, (m - hi.astype(np.float64)).astype(jnp.bfloat16)]))
+
+
+def middle_tree(part, leaves, digits, boxes):
+    c = 2 * R
+    bits = leaves.bit_length() - 1
+    first = digits.bit_length() - 1
+    total = boxes.bit_length() - 1 + bits
+    high = LANES.bit_length() - 1
+    n2 = high - high // 2
+    n3 = high - n2
+    own = digits // leaves
+    x = part.reshape(leaves, own, c, 2**n3, 2**n2)
+    x = x.transpose(4, 2, 0, 1, 3).reshape(2**n2 * c, -1)
+    x = mm(table(radix_matrix(first, n2)), x)
+    x = x.reshape(2**n2, c, leaves, own, 2**n3).transpose(4, 1, 2, 3, 0).reshape(2**n3 * c, -1)
+    x = mm(table(radix_matrix(first + n2, n3)), x)
+    x = x.reshape(2**n3, c, leaves, own * 2**n2).transpose(2, 1, 3, 0).reshape(leaves * c, -1)
+    x = mm(table(radix_matrix(total - bits, bits)), x)
+    return x.reshape(leaves, c, -1)
+
+
+def down_kernel(w_ref, tgt_hbm, a_hbm, out_hbm, tgt, out, a_buf, tab, coefs,
+                send, recv, gsend, grecv, tsem, asem, osem, *, leaves, blocks, depth, rows):
+    me, blk_no = lax.axis_index("leaf"), lax.axis_index("blk")
+    bits = leaves.bit_length() - 1
+    width = w_ref.shape[2]
+    tiles = width // LANES
+    cells = BOX_CELLS * 2**depth
+    ticks = TOP_TICKS // 2**depth
+    suffix = reverse_bits(me, bits)
+    across = lax.rem(blk_no + blocks // 2, blocks)
+    beside = blk_no + 1 - 2 * (blk_no % 2)
+    fetch = pltpu.make_async_copy(tgt_hbm, tgt, tsem)
+    load = pltpu.make_async_copy(a_hbm, a_buf, asem)
+    load.start()
+    fetch.start()
+
+    barrier = pltpu.get_barrier_semaphore()
+    for d in range(1, leaves):
+        pl.semaphore_signal(barrier, inc=1, device_id=(xor(me, d, bits), blk_no), device_id_type=pl.DeviceIdType.MESH)
+    for peer in (across, beside):
+        pl.semaphore_signal(barrier, inc=1, device_id=(me, peer), device_id_type=pl.DeviceIdType.MESH)
+    pl.semaphore_wait(barrier, leaves + 1)
+
+    def ship(d):
+        peer = xor(me, d, bits)
+        return pltpu.make_async_remote_copy(
+            src_ref=w_ref.at[reverse_bits(peer, bits)], dst_ref=coefs.at[blk_no, me],
+            send_sem=send.at[d - 1], recv_sem=recv.at[d - 1],
+            device_id=(peer, blk_no), device_id_type=pl.DeviceIdType.MESH,
+        )
+
+    def spread(way, d):
+        here = coefs.at[across if way == 2 else blk_no, xor(me, d, bits)]
+        return pltpu.make_async_remote_copy(
+            src_ref=here, dst_ref=here,
+            send_sem=gsend.at[way, d], recv_sem=grecv.at[way, d],
+            device_id=(me, across if way == 0 else beside), device_id_type=pl.DeviceIdType.MESH,
+        )
+
+    pitch = ticks // LANES
+    tilt = (blocks * cells - 1) / 2.0 * (pitch // 2) / 2.0**32
+    cos_poly = fit_even(lambda y: np.cos(2 * np.pi * y), tilt, 3)
+    sin_poly = fit_even(lambda y: np.sin(2 * np.pi * y) / y, tilt, 3)
+    cos_poly = [c * tilt ** (2 * k) for k, c in enumerate(cos_poly)]
+    sin_poly = [c * tilt ** (2 * k + 1) for k, c in enumerate(sin_poly)]
+    below = lax.broadcasted_iota(jnp.int32, (rows, LANES), 0) * (leaves * ticks)
+
+    def evaluate(chunk, t):
+        pack = jnp.concatenate([coefs[q, chunk, :, t * LANES : (t + 1) * LANES] for q in range(blocks)], axis=0)
+        hi, lo = split_pair(pack.T)
+        lhs = jnp.concatenate([hi, lo, hi], axis=1)
+        for n in range(2 * (DEGREE + 1)):
+            tab[t, n] = dot16(lhs, a_buf[:, n * LANES : (n + 1) * LANES])
+        first = pl.multiple_of(chunk * width + t * LANES, LANES)
+        for i in range(LANES // rows):
+            base = ((first + i * rows) * leaves + suffix) * ticks
+            u = (tgt[pl.ds(first + i * rows, rows), :] - (below + base)).astype(jnp.float32)
+            cell = (u * (1.0 / pitch) + (0.5 / pitch)).astype(jnp.int32)
+            s = (u - cell.astype(jnp.float32) * pitch) * (2.0 / pitch) - 1.0
+            got_at = [jnp.take_along_axis(tab[t, n, i * rows : (i + 1) * rows, :], cell, axis=1)
+                      for n in range(2 * (DEGREE + 1))]
+            z = s * s
+            powers = [None, s, z, z * s, z * z]
+            re, im = [[got_at[2 * p + part] * powers[p] if p else got_at[part] for p in range(DEGREE + 1)]
+                      for part in range(2)]
+            re = (re[0] + re[1]) + (re[2] + re[3]) + re[4]
+            im = (im[0] + im[1]) + (im[2] + im[3]) + im[4]
+            pc, ps = horner(cos_poly, z), s * horner(sin_poly, z)
+            out[pl.ds(2 * (first + i * rows), rows, stride=2), :] = pc * re - ps * im
+            out[pl.ds(2 * (first + i * rows) + 1, rows, stride=2), :] = pc * im + ps * re
+
+    def put(d):
+        span = pl.ds(pl.multiple_of(xor(me, d, bits) * (2 * width), 2 * width), 2 * width)
+        return pltpu.make_async_copy(out.at[span], out_hbm.at[span], osem.at[d])
+
+    order = [0] + far_first(leaves)
+    for d in order[1:]:
+        ship(d).start()
+    coefs[blk_no, me] = w_ref[suffix]
+    for step in range(leaves + 4):
+        if step < leaves:
+            d = order[step]
+            if d:
+                ship(d).wait_recv()
+            spread(0, d).start()
+            spread(1, d).start()
+        if 0 <= step - 4:
+            d = order[step - 4]
+            if step == 4:
+                load.wait()
+                fetch.wait()
+            spread(1, d).wait_recv()
+            spread(2, d).wait_recv()
+            for t in range(tiles):
+                evaluate(xor(me, d, bits), t)
+            put(d).start()
+        if 0 <= step - 2 < leaves:
+            d = order[step - 2]
+            spread(0, d).wait_recv()
+            spread(2, d).start()
+    for d in order:
+        if d:
+            ship(d).wait_send()
+        for way in range(3):
+            spread(way, d).wait_send()
+        put(d).wait()
+
+
+def down_call(weights, ticks, grid, leaves, blocks, depth):
+    boxes = ticks.shape[0]
+    width = boxes // leaves
+    whole = pl.BlockSpec(memory_space=pltpu.VMEM)
+    anywhere = pl.BlockSpec(memory_space=pl.ANY)
+    dma = pltpu.SemaphoreType.DMA
+    return pl.pallas_call(
+        functools.partial(down_kernel, leaves=leaves, blocks=blocks, depth=depth, rows=8),
+        out_shape=jax.ShapeDtypeStruct((2 * boxes, TGT_BOX), jnp.float32),
+        in_specs=[whole, anywhere, anywhere],
+        out_specs=anywhere,
+        scratch_shapes=[
+            pltpu.VMEM((boxes, TGT_BOX), jnp.int32),
+            pltpu.VMEM((2 * boxes, TGT_BOX), jnp.float32),
+            pltpu.VMEM(grid.shape, jnp.bfloat16),
+            pltpu.VMEM((width // LANES, 2 * (DEGREE + 1), LANES, LANES), jnp.float32),
+            pltpu.VMEM((blocks, leaves, 2 * R, width), jnp.float32),
+            dma((leaves - 1,)), dma((leaves - 1,)), dma((3, leaves)), dma((3, leaves)),
+            dma, dma, dma((leaves,)),
+        ],
+        compiler_params=pltpu.CompilerParams(collective_id=1, has_side_effects=True),
+        name="down",
+    )(weights, ticks, grid)
+
+
+def local_two_shuffles(src_pos, strengths, tgt_pos):
+    leaves, blocks = lax.axis_size("leaf"), lax.axis_size("blk")
+    boxes = src_pos.shape[1] // PER_BOX
+    depth = boxes.bit_length() - 1 + leaves.bit_length() - 1
+    part = up_call(src_pos.reshape(boxes, PER_BOX), strengths.reshape(2, boxes, PER_BOX), leaves)
+    weights = middle_tree(part, leaves, boxes // LANES, boxes)
+    grid = split_rows(grid_matrix(depth, blocks))
+    out = down_call(weights, tgt_pos.reshape(boxes, TGT_BOX), grid, leaves, blocks, depth)
+    return out.reshape(boxes, 2, TGT_BOX).transpose(1, 0, 2).reshape(2, boxes * TGT_BOX)
+
+
 def solution(mesh):
+    def local(src_pos, strengths, tgt_pos):
+        boxes = src_pos.shape[1] // PER_BOX
+        near = mesh.shape["leaf"] * LANES <= boxes and mesh.shape["blk"] == 4
+        run = local_two_shuffles if near else local_butterfly
+        return run(src_pos, strengths, tgt_pos)
+
     return jax.shard_map(
         local,
         mesh=mesh,

time: 71 us -> 55.2 us (0.78)
  Pallas kernels: 60.7 us -> 44 us
  local copies, waits for them, and re-layouts: 6.18 us -> 8.07 us
  matrix products: 3.76 us -> 2.73 us
    pallas_call x2, Pallas kernels: 60.7 us -> 44 us  [the longest x1 23.4 us: up_call(): pl.pallas_call(functools.partial(up_kernel, digits=digits, leaves=leaves)...]
    pallas_call x0 -> x1, local copies, waits for them, and re-layouts: none -> 1.15 us  [up_call(): pl.pallas_call(functools.partial(up_kernel, digits=digits, leaves=leaves)...]
    dot_general x3, matrix products: 3.76 us -> 2.73 us  [mm(): return jnp.dot(a, b, precision=HIGHEST, preferred_element_type=jnp.float32)]
    reshape x6 -> x7, local copies, waits for them, and re-layouts: 2.7 us -> 3.16 us  [the longest x3 1.55 us: middle_tree(): x.reshape(2 ** n3, c, leaves, own * 2 ** n2).transpose(2, 1, 3, 0)]
where the time goes in v2:
time: 55.2 us; the launch traced here: 55 us
  Pallas kernels  44 us (80%)
  local copies, waits for them, and re-layouts  8.07 us (15%)
  matrix products  2.73 us (5%)
    pallas_call x1, Pallas kernels, up_call(): pl.pallas_call(functools.partial(up_kernel, digits=digits, leaves=leaves)...  23.4 us
    pallas_call x1, Pallas kernels, down_call(): pl.pallas_call(functools.partial(down_kernel, leaves=leaves, blocks=block...  20.7 us
    unnamed x7, local copies, waits for them, and re-layouts  3.31 us
    dot_general x3, matrix products, mm(): return jnp.dot(a, b, precision=HIGHEST, preferred_element_type=jnp.float32)  2.73 us
    reshape x3, local copies, waits for them, and re-layouts, middle_tree(): x.reshape(2 ** n3, c, leaves, own * 2 ** n2).transpose(2, 1, 3, 0)  1.55 us
    pallas_call x1, local copies, waits for them, and re-layouts, up_call(): pl.pallas_call(functools.partial(up_kernel, digits=digits, leaves=leaves)...  1.15 us

profile of v2, /device:TPU:0, one launch (start us, length us, event | category | flops | bytes accessed | tf_op | source)
XLA Modules:
  0.0 55.0 jit_solution(3058897299077252335)
XLA Ops:
  0.0 23.4 %up.1 = f32[8,64,128]{2,1,0:T(8,128)} custom-call(s32[2048,128]{1,0:T(8,128)} %bitcast.39, f32[2,2048,128]{2,1,0:T(8,128)} %bitcast.38, f32[32,256]{1,0:T(8,128)} %constant.12.clone.mix_ref, bf16[2,512,512]{2,1,0:T(8,128)(2,1)} %constant.13.clone.w_hbm), custom_call_target="tpu_custom_call" | custom-call | tf_op jit(solution)/shard_map/up/pallas_call | solution.py:479
  23.4 1.1 %copy.11 = f32[8,64,128]{1,2,0:T(8,128)S(1)} copy(f32[8,64,128]{2,1,0:T(8,128)} %up.1) | data formatting | bytes 524288 | tf_op jit(solution)/shard_map/up/pallas_call | solution.py:479
  24.5 0.6 %reshape.38 = f32[8,2,32,8,16]{2,1,4,3,0:T(2,128)S(1)} reshape(f32[8,64,128]{1,2,0:T(8,128)S(1)} %copy.11) | data formatting | bytes 524288 | tf_op jit(solution)/shard_map/reshape | solution.py:513
  25.1 0.0 copy-start
  25.2 0.1 copy.12
  25.3 0.4 reshape.39
  25.7 0.7 %copy-done = f32[512,512]{1,0:T(8,128)S(1)} copy-done((f32[512,512]{1,0:T(8,128)S(1)}, f32[512,512]{1,0:T(8,128)}, u32[]{:S(2)}) %copy-start) | copy-done | bytes 1048600
  26.4 1.2 %fusion = f32[512,128]{0,1:T(8,128)S(1)} fusion(f32[512,512]{1,0:T(8,128)S(1)} %copy-done, f32[512,128]{0,1:T(8,128)S(1)} %reshape.39), kind=kOutput, calls=%fused_computation | convolution fusion | flops 402653184 | bytes 1572864 | tf_op jit(solution)/shard_map/dot_general | solution.py:379
  27.6 0.0 copy-start.2
  27.6 0.3 reshape.40
  27.9 0.3 copy.14
  28.2 0.3 reshape.41
  28.5 0.0 copy-done.2
  28.6 0.4 fusion.1
  29.0 0.0 copy-start.1
  29.0 0.3 reshape.42
  29.3 1.0 %copy.15 = f32[8,32,8,32]{1,2,0,3:T(8,128)S(1)} copy(f32[8,32,8,32]{3,2,1,0:T(8,128)S(1)} %reshape.42) | data formatting | bytes 524288 | tf_op jit(solution)/shard_map/reshape | solution.py:518
  30.2 0.3 reshape.43
  30.6 0.0 copy-done.1
  30.6 1.1 %fusion.2 = f32[256,256]{1,0:T(8,128)} fusion(f32[256,256]{1,0:T(8,128)S(1)} %copy-done.1, f32[256,256]{0,1:T(8,128)S(1)} %reshape.43), kind=kOutput, calls=%fused_computation.2 | convolution fusion | flops 201326592 | bytes 786432 | tf_op jit(solution)/shard_map/dot_general | solution.py:379
  31.7 20.7 %down.1 = f32[4096,128]{1,0:T(8,128)} custom-call(f32[8,32,256]{2,1,0:T(8,128)} %bitcast.40, s32[2048,128]{1,0:T(8,128)} %bitcast.41, bf16[384,1280]{1,0:T(8,128)(2,1)} %constant.17.clone.a_hbm), custom_call_target="tpu_custom_call" | custom-call | tf_op jit(solution)/shard_map/down/pallas_call | solution.py:637
  52.4 2.6 %copy.19 = f32[2,262144]{1,0:T(2,128)} copy(f32[2,262144]{1,0:T(2,128)} %bitcast.34) | data formatting | bytes 4194304
Async XLA Ops:
  25.1 1.2 %copy-start = (f32[512,512]{1,0:T(8,128)S(1)}, f32[512,512]{1,0:T(8,128)}, u32[]{:S(2)}) copy-start(f32[512,512]{1,0:T(8,128)} %constant.14.clone) | copy-start | bytes 3145732
  27.6 1.0 %copy-start.2 = (f32[256,256]{1,0:T(8,128)S(1)}, f32[256,256]{1,0:T(8,128)}, u32[]{:S(2)}) copy-start(f32[256,256]{1,0:T(8,128)} %constant.15.clone) | copy-start | bytes 786436
  29.0 1.6 %copy-start.1 = (f32[256,256]{1,0:T(8,128)S(1)}, f32[256,256]{1,0:T(8,128)}, u32[]{:S(2)}) copy-start(f32[256,256]{1,0:T(8,128)} %constant.16.clone) | copy-start | bytes 786436

commit v3 on v1

--- a/solution.py
+++ b/solution.py
@@ -394,7 +394,7 @@
     return y.reshape(2**n3, c, low * 2**n2).transpose(1, 2, 0).reshape(c, boxes)
 
 
-def local(src_pos, strengths, tgt_pos):
+def local_butterfly(src_pos, strengths, tgt_pos):
     leaf_count = lax.axis_size("leaf")
     leaf_bits = leaf_count.bit_length() - 1
     boxes = src_pos.shape[1] // PER_BOX
@@ -412,7 +412,371 @@
     return out.reshape(boxes, 2, TGT_BOX).transpose(1, 0, 2).reshape(2, boxes * TGT_BOX)
 
 
+def xor(a, d, bits):
+    return sum(((a // 2**k % 2 + (d >> k) % 2) % 2) * 2**k for k in range(bits))
+
+
+def reverse_bits(a, bits):
+    return sum((a // 2**k % 2) * 2 ** (bits - 1 - k) for k in range(bits))
+
+
+def split_pair(x):
+    hi = x.astype(jnp.bfloat16)
+    return hi, (x - hi.astype(jnp.float32)).astype(jnp.bfloat16)
+
+
+def dot16(a, b):
+    return jnp.dot(a, b, preferred_element_type=jnp.float32)
+
+
+def far_first(leaves):
+    half = leaves // 2
+    return [1] + list(range(half, leaves)) + list(range(2, half)) if leaves > 2 else [1]
+
+
+def two_parts(m):
+    hi = m.astype(jnp.bfloat16)
+    return jnp.asarray(np.stack([hi, (m - hi.astype(np.float64)).astype(jnp.bfloat16)]))
+
+
+def moment_matrix():
+    wide = leaf_matrix()
+    g = wide[:R, : 8 * R : 8].astype(np.float64)
+    half = R // 2
+    q = np.zeros((R, R))
+    for n in range(half):
+        q[n, n] = 1.0
+        q[half + n, half + n] = 2.0 if n else 1.0
+        if n:
+            q[half + n, half - n] = -1.0
+    return np.kron(np.eye(2), g @ q)
+
+
+def first_matrix(count):
+    m = radix_matrix(0, count)
+    return np.einsum("xbc,cd->xbd", m.reshape(m.shape[0], -1, 2 * R), moment_matrix()).reshape(m.shape)
+
+
+def merge_rows(parts):
+    row = lax.broadcasted_iota(jnp.int32, (8, LANES), 0)
+    step = 1
+    while len(parts) > 1:
+        low = row // step % 2 == 0
+        half = len(parts) // 2
+        pairs = [(parts[2 * k], parts[2 * k + 1]) for k in range(half)]
+        parts = [jnp.where(low, a, b) + pltpu.roll(jnp.where(low, b, a), step, 0) for a, b in pairs]
+        step *= 2
+    return parts[0]
+
+
+def swap_bits(slots, pairs):
+    lane = lax.broadcasted_iota(jnp.int32, (8, LANES), 1)
+    slots = list(slots)
+    for slot_bit, lane_bit in pairs:
+        low = lane // 2**lane_bit % 2 == 0
+        for k in range(len(slots)):
+            if k >> slot_bit & 1 == 0:
+                a, b = slots[k], slots[k + 2**slot_bit]
+                slots[k] = jnp.where(low, a, pltpu.roll(b, 2**lane_bit, 1))
+                slots[k + 2**slot_bit] = jnp.where(low, pltpu.roll(a, LANES - 2**lane_bit, 1), b)
+    return slots
+
+
+def mm3(w, x):
+    hi, lo = split_pair(x)
+    return dot16(w[0], hi) + dot16(w[0], lo) + dot16(w[1], hi)
+
+
+def whole_kernel(pos_hbm, str_hbm, w1_hbm, w2_hbm, w3_hbm, w4_hbm, a_hbm, tgt_hbm, out_hbm,
+                 pos, amp, p_t, re_t, im_t, stack, w1, w2, w3, w4, y, got, x2, x3, x4, mine,
+                 tgt, out, a_buf, tab, coefs,
+                 isem, wsem, send1, recv1, send, recv, gsend, grecv, osem,
+                 *, digits, leaves, blocks, depth, rows):
+    me, blk_no = lax.axis_index("leaf"), lax.axis_index("blk")
+    bits = leaves.bit_length() - 1
+    own = digits // leaves
+    mesh_id = pl.DeviceIdType.MESH
+    across = lax.rem(blk_no + blocks // 2, blocks)
+    beside = blk_no + 1 - 2 * (blk_no % 2)
+    groups = digits // 8
+
+    def take(g):
+        return [
+            pltpu.make_async_copy(pos_hbm.at[:, g], pos.at[g], isem.at[0, g]),
+            pltpu.make_async_copy(str_hbm.at[0, :, g], amp.at[0, g], isem.at[1, g]),
+            pltpu.make_async_copy(str_hbm.at[1, :, g], amp.at[1, g], isem.at[2, g]),
+        ]
+
+    later = [
+        pltpu.make_async_copy(src, dst, wsem.at[k])
+        for k, (src, dst) in enumerate([(w1_hbm, w1), (w2_hbm, w2), (w3_hbm, w3), (w4_hbm, w4), (a_hbm, a_buf), (tgt_hbm, tgt)])
+    ]
+    for g in range(groups):
+        for copy in take(g):
+            copy.start()
+    for copy in later:
+        copy.start()
+    barrier = pltpu.get_barrier_semaphore()
+    for d in range(1, leaves):
+        pl.semaphore_signal(barrier, inc=1, device_id=(xor(me, d, bits), blk_no), device_id_type=mesh_id)
+    for peer in (across, beside):
+        pl.semaphore_signal(barrier, inc=1, device_id=(me, peer), device_id_type=mesh_id)
+
+    cells_at = lax.broadcasted_iota(jnp.int32, (8, LANES), 1)
+    cos_at, sin_at = cos_sin_turns((cells_at * (TOP_TICKS // 2)).astype(jnp.float32) * (2.0**-32))
+
+    def turn_over(g, beta, slot):
+        here = pl.ds(beta, LANES, stride=8)
+        p_t[slot] = pos.reshape(groups, LANES * 8, LANES)[g, here, :].T
+        re_t[slot] = amp.reshape(2, groups, LANES * 8, LANES)[0, g, here, :].T
+        im_t[slot] = amp.reshape(2, groups, LANES * 8, LANES)[1, g, here, :].T
+
+    def chunk(slot, i, acc):
+        here = pl.ds(i * 8, 8)
+        r = p_t[slot, here, :] & (BOX_CELLS - 1)
+        c = jnp.take_along_axis(cos_at, r, axis=1)
+        s = jnp.take_along_axis(sin_at, r, axis=1)
+        a, b = re_t[slot, here, :], im_t[slot, here, :]
+        v = r.astype(jnp.float32) * (2.0 / BOX_CELLS) - 1.0
+        v2 = v + v
+        cheb = [None, v]
+        for k in range(2, R // 2 + 1):
+            cheb.append(v2 * v - 1.0 if k == 2 else v2 * cheb[-1] - cheb[-2])
+        x, z = c * a - s * b, s * a + c * b
+        result = []
+        for part, (x, z) in enumerate([(x, z), (cheb[-1] * x, cheb[-1] * z)]):
+            for k in range(R // 2):
+                u, w = acc[part * (R // 2) + k]
+                result.append((u + x, w + z) if k == 0 else (u + cheb[k] * x, w + cheb[k] * z))
+        return tuple(result)
+
+    for g in range(groups):
+        for copy in take(g):
+            copy.wait()
+        turn_over(g, 0, 0)
+
+        def tile(beta, carry, g=g):
+            slot = lax.rem(beta, 2)
+            turn_over(g, jnp.minimum(beta + 1, 7), 1 - slot)
+            zero = jnp.zeros((8, LANES), jnp.float32)
+            acc = tuple((zero, zero) for _ in range(R))
+            for i in range(PER_BOX // 8):
+                acc = chunk(slot, i, acc)
+            half = R // 2
+            for part in range(2):
+                for k in range(2):
+                    stack[g * 8 + beta, (2 * part + k) * 8 : (2 * part + k + 1) * 8, :] = merge_rows(
+                        [acc[k * half + n][part] for n in range(half)])
+            return carry
+
+        lax.fori_loop(0, 8, tile, 0)
+
+    later[0].wait()
+    y[...] = mm3(w1, stack[...].reshape(digits * 2 * R, LANES)).reshape(y.shape)
+    pl.semaphore_wait(barrier, leaves + 1)
+
+    def shuffle(d):
+        peer = xor(me, d, bits)
+        return pltpu.make_async_remote_copy(
+            src_ref=y.at[peer], dst_ref=got.at[me],
+            send_sem=send1.at[d - 1], recv_sem=recv1.at[d - 1],
+            device_id=(peer, blk_no), device_id_type=mesh_id,
+        )
+
+    for d in far_first(leaves):
+        shuffle(d).start()
+    got[me] = y[me]
+    for d in far_first(leaves):
+        shuffle(d).wait_recv()
+
+    n2, n3 = digits.bit_length() - 1, LANES.bit_length() - digits.bit_length()
+    for cg in range(2 * R // 8):
+        slots = [got[k, a * 2 * R + cg * 8 : a * 2 * R + cg * 8 + 8, :] for a in range(own) for k in range(leaves)]
+        slots = swap_bits(slots, [(k, k) for k in range(n2)])
+        for k, v in enumerate(slots):
+            x2[k * 2 * R + cg * 8 : k * 2 * R + cg * 8 + 8, :] = v
+    later[1].wait()
+    z2 = mm3(w2, x2[...])
+    x2[...] = z2
+    for cg in range(2 * R // 8):
+        slots = [x2[k * 2 * R + cg * 8 : k * 2 * R + cg * 8 + 8, :] for k in range(digits)]
+        slots = swap_bits(slots, [(k, n3 + k) for k in range(n2)])
+        for k, v in enumerate(slots):
+            x3[k // own * 2 * R + cg * 8 : k // own * 2 * R + cg * 8 + 8, k % own * LANES : (k % own + 1) * LANES] = v
+    later[2].wait()
+    x4[...] = mm3(w3, x3[...])
+    for cg in range(2 * R // 8):
+        for a in range(own):
+            cols = slice(a * LANES, (a + 1) * LANES)
+            slots = [x4[k * 2 * R + cg * 8 : k * 2 * R + cg * 8 + 8, cols] for k in range(leaves)]
+            slots = swap_bits(slots, [(k, k) for k in range(n3)])
+            for k, v in enumerate(slots):
+                x3[k * 2 * R + cg * 8 : k * 2 * R + cg * 8 + 8, cols] = v
+    later[3].wait()
+    z4 = mm3(w4, x3[...])
+    for a in range(own):
+        mine[:, a] = z4[:, a * LANES : (a + 1) * LANES].reshape(leaves, 2 * R, LANES)
+
+    width = own * LANES
+    cells = BOX_CELLS * 2**depth
+    ticks = TOP_TICKS // 2**depth
+    suffix = reverse_bits(me, bits)
+
+    def ship(d):
+        peer = xor(me, d, bits)
+        return pltpu.make_async_remote_copy(
+            src_ref=mine.at[reverse_bits(peer, bits)], dst_ref=coefs.at[blk_no, me],
+            send_sem=send.at[d - 1], recv_sem=recv.at[d - 1],
+            device_id=(peer, blk_no), device_id_type=mesh_id,
+        )
+
+    def spread(way, d):
+        here = coefs.at[across if way == 2 else blk_no, xor(me, d, bits)]
+        return pltpu.make_async_remote_copy(
+            src_ref=here, dst_ref=here,
+            send_sem=gsend.at[way, d], recv_sem=grecv.at[way, d],
+            device_id=(me, across if way == 0 else beside), device_id_type=mesh_id,
+        )
+
+    pitch = ticks // LANES
+    tilt = (blocks * cells - 1) / 2.0 * (pitch // 2) / 2.0**32
+    cos_poly = fit_even(lambda y: np.cos(2 * np.pi * y), tilt, 3)
+    sin_poly = fit_even(lambda y: np.sin(2 * np.pi * y) / y, tilt, 3)
+    cos_poly = [c * tilt ** (2 * k) for k, c in enumerate(cos_poly)]
+    sin_poly = [c * tilt ** (2 * k + 1) for k, c in enumerate(sin_poly)]
+    below = lax.broadcasted_iota(jnp.int32, (rows, LANES), 0) * (leaves * ticks)
+
+    def evaluate(chunk, t):
+        pack = jnp.concatenate([coefs[q, chunk, t] for q in range(blocks)], axis=0)
+        hi, lo = split_pair(pack.T)
+        lhs = jnp.concatenate([hi, lo, hi], axis=1)
+        for n in range(2 * (DEGREE + 1)):
+            tab[t, n] = dot16(lhs, a_buf[:, n * LANES : (n + 1) * LANES])
+        first = pl.multiple_of(chunk * width + t * LANES, LANES)
+        for i in range(LANES // rows):
+            base = ((first + i * rows) * leaves + suffix) * ticks
+            u = (tgt[pl.ds(first + i * rows, rows), :] - (below + base)).astype(jnp.float32)
+            cell = (u * (1.0 / pitch) + (0.5 / pitch)).astype(jnp.int32)
+            s = (u - cell.astype(jnp.float32) * pitch) * (2.0 / pitch) - 1.0
+            got_at = [jnp.take_along_axis(tab[t, n, i * rows : (i + 1) * rows, :], cell, axis=1)
+                      for n in range(2 * (DEGREE + 1))]
+            z = s * s
+            powers = [None, s, z, z * s, z * z]
+            re, im = [[got_at[2 * p + part] * powers[p] if p else got_at[part] for p in range(DEGREE + 1)]
+                      for part in range(2)]
+            re = (re[0] + re[1]) + (re[2] + re[3]) + re[4]
+            im = (im[0] + im[1]) + (im[2] + im[3]) + im[4]
+            pc, ps = horner(cos_poly, z), s * horner(sin_poly, z)
+            out[pl.ds(2 * (first + i * rows), rows, stride=2), :] = pc * re - ps * im
+            out[pl.ds(2 * (first + i * rows) + 1, rows, stride=2), :] = pc * im + ps * re
+
+    def put(d):
+        span = pl.ds(pl.multiple_of(xor(me, d, bits) * (2 * width), 2 * width), 2 * width)
+        return pltpu.make_async_copy(out.at[span], out_hbm.at[span], osem.at[d])
+
+    order = [0] + far_first(leaves)
+    for d in order[1:]:
+        ship(d).start()
+    coefs[blk_no, me] = mine[suffix]
+    for step in range(leaves + 4):
+        if step < leaves:
+            d = order[step]
+            if d:
+                ship(d).wait_recv()
+            spread(0, d).start()
+            spread(1, d).start()
+        if 0 <= step - 4:
+            d = order[step - 4]
+            if step == 4:
+                later[4].wait()
+                later[5].wait()
+            spread(1, d).wait_recv()
+            spread(2, d).wait_recv()
+            for t in range(own):
+                evaluate(xor(me, d, bits), t)
+            put(d).start()
+        if 0 <= step - 2 < leaves:
+            d = order[step - 2]
+            spread(0, d).wait_recv()
+            spread(2, d).start()
+    for d in order:
+        if d:
+            shuffle(d).wait_send()
+            ship(d).wait_send()
+        for way in range(3):
+            spread(way, d).wait_send()
+        put(d).wait()
+
+
+def whole_call(pos, strengths, ticks, leaves, blocks, depth):
+    boxes = ticks.shape[0]
+    digits = boxes // LANES
+    groups = digits // 8
+    own = digits // leaves
+    n1 = digits.bit_length() - 1
+    n3 = LANES.bit_length() - digits.bit_length()
+    n, m = digits * 2 * R, 2**n3 * 2 * R
+    grid = split_rows(grid_matrix(depth, blocks))
+    anywhere = pl.BlockSpec(memory_space=pl.ANY)
+    dma = pltpu.SemaphoreType.DMA
+    f32, bf16 = jnp.float32, jnp.bfloat16
+    return pl.pallas_call(
+        functools.partial(whole_kernel, digits=digits, leaves=leaves, blocks=blocks, depth=depth, rows=8),
+        out_shape=jax.ShapeDtypeStruct((2 * boxes, TGT_BOX), f32),
+        in_specs=[anywhere] * 8,
+        out_specs=anywhere,
+        scratch_shapes=[
+            pltpu.VMEM((groups, LANES, 8, LANES), jnp.int32),
+            pltpu.VMEM((2, groups, LANES, 8, LANES), f32),
+            pltpu.VMEM((2, LANES, LANES), jnp.int32),
+            pltpu.VMEM((2, LANES, LANES), f32),
+            pltpu.VMEM((2, LANES, LANES), f32),
+            pltpu.VMEM((digits, 2 * R, LANES), f32),
+            pltpu.VMEM((2, n, n), bf16),
+            pltpu.VMEM((2, n, n), bf16),
+            pltpu.VMEM((2, m, m), bf16),
+            pltpu.VMEM((2, m, m), bf16),
+            pltpu.VMEM((leaves, n // leaves, LANES), f32),
+            pltpu.VMEM((leaves, n // leaves, LANES), f32),
+            pltpu.VMEM((n, LANES), f32),
+            pltpu.VMEM((m, own * LANES), f32),
+            pltpu.VMEM((m, own * LANES), f32),
+            pltpu.VMEM((leaves, own, 2 * R, LANES), f32),
+            pltpu.VMEM((boxes, TGT_BOX), jnp.int32),
+            pltpu.VMEM((2 * boxes, TGT_BOX), f32),
+            pltpu.VMEM(grid.shape, bf16),
+            pltpu.VMEM((own, 2 * (DEGREE + 1), LANES, LANES), f32),
+            pltpu.VMEM((blocks, leaves, own, 2 * R, LANES), f32),
+            dma((3, groups)), dma((6,)), dma((leaves - 1,)), dma((leaves - 1,)),
+            dma((leaves - 1,)), dma((leaves - 1,)), dma((3, leaves)), dma((3, leaves)), dma((leaves,)),
+        ],
+        compiler_params=pltpu.CompilerParams(collective_id=0, has_side_effects=True),
+        name="whole",
+    )(
+        pos.reshape(LANES, groups, 8, LANES), strengths.reshape(2, LANES, groups, 8, LANES),
+        two_parts(first_matrix(n1)), two_parts(radix_matrix(n1, n1)),
+        two_parts(radix_matrix(2 * n1, n3)), two_parts(radix_matrix(2 * n1 + n3, n3)),
+        grid, ticks,
+    )
+
+
+def local_two_shuffles(src_pos, strengths, tgt_pos):
+    leaves, blocks = lax.axis_size("leaf"), lax.axis_size("blk")
+    boxes = src_pos.shape[1] // PER_BOX
+    depth = boxes.bit_length() - 1 + leaves.bit_length() - 1
+    out = whole_call(src_pos, strengths, tgt_pos.reshape(boxes, TGT_BOX), leaves, blocks, depth)
+    return out.reshape(boxes, 2, TGT_BOX).transpose(1, 0, 2).reshape(2, boxes * TGT_BOX)
+
+
 def solution(mesh):
+    def local(src_pos, strengths, tgt_pos):
+        boxes = src_pos.shape[1] // PER_BOX
+        digits = boxes // LANES
+        fits = digits % 8 == 0 and digits == 2 * mesh.shape["leaf"] and mesh.shape["leaf"] * digits == LANES
+        near = fits and mesh.shape["blk"] == 4
+        run = local_two_shuffles if near else local_butterfly
+        return run(src_pos, strengths, tgt_pos)
+
     return jax.shard_map(
         local,
         mesh=mesh,

time: 71 us -> 43.2 us (0.61)
  Pallas kernels: 60.7 us -> 40.4 us
  matrix products: 3.76 us -> 0 us
  local copies, waits for them, and re-layouts: 6.18 us -> 2.61 us
    pallas_call x2 -> x1, Pallas kernels: 60.7 us -> 40.4 us  [whole_call(): pl.pallas_call(functools.partial(whole_kernel, digits=digits, leaves=leav...]
    dot_general x3 -> x0, matrix products: 3.76 us -> none  [mm(): return jnp.dot(a, b, precision=HIGHEST, preferred_element_type=jnp.float32)]
    reshape x6 -> x0, local copies, waits for them, and re-layouts: 2.7 us -> none  [the longest x2 1.43 us: local_tree(): y.reshape(2 ** n3, c, low * 2 ** n2).transpose(1, 2, 0).reshape(c, boxes)]
    unnamed x7 -> x1, local copies, waits for them, and re-layouts: 2.79 us -> 2.61 us
where the time goes in v3:
time: 43.2 us; the launch traced here: 43 us
  Pallas kernels  40.4 us (94%)
  local copies, waits for them, and re-layouts  2.61 us (6%)
    pallas_call x1, Pallas kernels, whole_call(): pl.pallas_call(functools.partial(whole_kernel, digits=digits, leaves=leav...  40.4 us
    unnamed x1, local copies, waits for them, and re-layouts  2.61 us

profile of v3, /device:TPU:0, one launch (start us, length us, event | category | flops | bytes accessed | tf_op | source)
XLA Modules:
  0.0 43.0 jit_solution(17770370150491945621)
XLA Ops:
  0.0 40.4 %whole.1 = f32[4096,128]{1,0:T(8,128)} custom-call(s32[128,2,8,128]{3,2,1,0:T(8,128)} %bitcast.10, f32[2,128,2,8,128]{4,3,2,1,0:T(8,128)} %bitcast.9, bf16[2,512,512]{2,1,0:T(8,128)(2,1)} %constant.11.clone.w1_hbm, bf16[2,512,512]{2,1,0:T(8,128)(2,1)} %constant.12.clone.w2_hbm, bf16[2,256,256]{2,1,0:T(8,128)(2,1)} %constant.13.clone.w3_hbm, ...), custom_call_target="tpu_custom_call" | custom-call | tf_op jit(solution)/shard_map/whole/pallas_call | solution.py:723
  40.4 2.6 %copy.11 = f32[2,262144]{1,0:T(2,128)} copy(f32[2,262144]{1,0:T(2,128)} %bitcast.8) | data formatting | bytes 4194304

commit v4 on v3

--- a/solution.py
+++ b/solution.py
@@ -514,13 +514,10 @@
     for g in range(groups):
         for copy in take(g):
             copy.start()
-    for copy in later:
-        copy.start()
     barrier = pltpu.get_barrier_semaphore()
-    for d in range(1, leaves):
-        pl.semaphore_signal(barrier, inc=1, device_id=(xor(me, d, bits), blk_no), device_id_type=mesh_id)
-    for peer in (across, beside):
-        pl.semaphore_signal(barrier, inc=1, device_id=(me, peer), device_id_type=mesh_id)
+    for d in range(leaves):
+        for peer in (blk_no, across) if d else (beside, across):
+            pl.semaphore_signal(barrier, inc=1, device_id=(xor(me, d, bits), peer), device_id_type=mesh_id)
 
     cells_at = lax.broadcasted_iota(jnp.int32, (8, LANES), 1)
     cos_at, sin_at = cos_sin_turns((cells_at * (TOP_TICKS // 2)).astype(jnp.float32) * (2.0**-32))
@@ -553,6 +550,9 @@
     for g in range(groups):
         for copy in take(g):
             copy.wait()
+        if g == 0:
+            for copy in later:
+                copy.start()
         turn_over(g, 0, 0)
 
         def tile(beta, carry, g=g):
@@ -573,7 +573,7 @@
 
     later[0].wait()
     y[...] = mm3(w1, stack[...].reshape(digits * 2 * R, LANES)).reshape(y.shape)
-    pl.semaphore_wait(barrier, leaves + 1)
+    pl.semaphore_wait(barrier, 2 * leaves)
 
     def shuffle(d):
         peer = xor(me, d, bits)
@@ -622,20 +622,20 @@
     ticks = TOP_TICKS // 2**depth
     suffix = reverse_bits(me, bits)
 
-    def ship(d):
+    def ship(way, d):
         peer = xor(me, d, bits)
         return pltpu.make_async_remote_copy(
             src_ref=mine.at[reverse_bits(peer, bits)], dst_ref=coefs.at[blk_no, me],
-            send_sem=send.at[d - 1], recv_sem=recv.at[d - 1],
-            device_id=(peer, blk_no), device_id_type=mesh_id,
+            send_sem=send.at[way, d], recv_sem=recv.at[way, d],
+            device_id=(peer, across if way else blk_no), device_id_type=mesh_id,
         )
 
-    def spread(way, d):
-        here = coefs.at[across if way == 2 else blk_no, xor(me, d, bits)]
+    def forward(way, d):
+        here = coefs.at[across if way else blk_no, xor(me, d, bits)]
         return pltpu.make_async_remote_copy(
             src_ref=here, dst_ref=here,
             send_sem=gsend.at[way, d], recv_sem=grecv.at[way, d],
-            device_id=(me, across if way == 0 else beside), device_id_type=mesh_id,
+            device_id=(me, beside), device_id_type=mesh_id,
         )
 
     pitch = ticks // LANES
@@ -646,19 +646,23 @@
     sin_poly = [c * tilt ** (2 * k + 1) for k, c in enumerate(sin_poly)]
     below = lax.broadcasted_iota(jnp.int32, (rows, LANES), 0) * (leaves * ticks)
 
-    def evaluate(chunk, t):
-        pack = jnp.concatenate([coefs[q, chunk, t] for q in range(blocks)], axis=0)
-        hi, lo = split_pair(pack.T)
+    def tables(chunk, slot):
+        parts = [split_pair(jnp.concatenate([coefs[q, chunk, t] for q in range(blocks)], axis=0).T) for t in range(own)]
+        hi, lo = [jnp.concatenate(part, axis=0) for part in zip(*parts)]
         lhs = jnp.concatenate([hi, lo, hi], axis=1)
-        for n in range(2 * (DEGREE + 1)):
-            tab[t, n] = dot16(lhs, a_buf[:, n * LANES : (n + 1) * LANES])
-        first = pl.multiple_of(chunk * width + t * LANES, LANES)
-        for i in range(LANES // rows):
+        for p in range(DEGREE + 1):
+            both = dot16(lhs, a_buf[:, 2 * p * LANES : 2 * (p + 1) * LANES])
+            tab[slot, 2 * p] = both[:, :LANES]
+            tab[slot, 2 * p + 1] = both[:, LANES:]
+
+    def points(chunk, slot):
+        first = pl.multiple_of(chunk * width, width)
+        for i in range(width // rows):
             base = ((first + i * rows) * leaves + suffix) * ticks
             u = (tgt[pl.ds(first + i * rows, rows), :] - (below + base)).astype(jnp.float32)
             cell = (u * (1.0 / pitch) + (0.5 / pitch)).astype(jnp.int32)
             s = (u - cell.astype(jnp.float32) * pitch) * (2.0 / pitch) - 1.0
-            got_at = [jnp.take_along_axis(tab[t, n, i * rows : (i + 1) * rows, :], cell, axis=1)
+            got_at = [jnp.take_along_axis(tab[slot, n, i * rows : (i + 1) * rows, :], cell, axis=1)
                       for n in range(2 * (DEGREE + 1))]
             z = s * s
             powers = [None, s, z, z * s, z * z]
@@ -675,36 +679,37 @@
         return pltpu.make_async_copy(out.at[span], out_hbm.at[span], osem.at[d])
 
     order = [0] + far_first(leaves)
-    for d in order[1:]:
-        ship(d).start()
+    both = [(way, d) for d in order for way in range(2) if way or d]
+    for way, d in both:
+        ship(way, d).start()
     coefs[blk_no, me] = mine[suffix]
-    for step in range(leaves + 4):
+    lag = 2
+    for step in range(leaves + lag + 1):
         if step < leaves:
             d = order[step]
-            if d:
-                ship(d).wait_recv()
-            spread(0, d).start()
-            spread(1, d).start()
-        if 0 <= step - 4:
-            d = order[step - 4]
-            if step == 4:
-                later[4].wait()
-                later[5].wait()
-            spread(1, d).wait_recv()
-            spread(2, d).wait_recv()
-            for t in range(own):
-                evaluate(xor(me, d, bits), t)
+            for way in range(2):
+                if way or d:
+                    ship(way, d).wait_recv()
+                forward(way, d).start()
+        if step == lag:
+            later[4].wait()
+            later[5].wait()
+        if 0 <= step - lag < leaves:
+            d = order[step - lag]
+            for way in range(2):
+                forward(way, d).wait_recv()
+            tables(xor(me, d, bits), (step - lag) % 2)
+        if 0 <= step - lag - 1:
+            d = order[step - lag - 1]
+            points(xor(me, d, bits), (step - lag - 1) % 2)
             put(d).start()
-        if 0 <= step - 2 < leaves:
-            d = order[step - 2]
-            spread(0, d).wait_recv()
-            spread(2, d).start()
     for d in order:
         if d:
             shuffle(d).wait_send()
-            ship(d).wait_send()
-        for way in range(3):
-            spread(way, d).wait_send()
+        for way in range(2):
+            if way or d:
+                ship(way, d).wait_send()
+            forward(way, d).wait_send()
         put(d).wait()
 
 
@@ -745,10 +750,10 @@
             pltpu.VMEM((boxes, TGT_BOX), jnp.int32),
             pltpu.VMEM((2 * boxes, TGT_BOX), f32),
             pltpu.VMEM(grid.shape, bf16),
-            pltpu.VMEM((own, 2 * (DEGREE + 1), LANES, LANES), f32),
+            pltpu.VMEM((2, 2 * (DEGREE + 1), own * LANES, LANES), f32),
             pltpu.VMEM((blocks, leaves, own, 2 * R, LANES), f32),
             dma((3, groups)), dma((6,)), dma((leaves - 1,)), dma((leaves - 1,)),
-            dma((leaves - 1,)), dma((leaves - 1,)), dma((3, leaves)), dma((3, leaves)), dma((leaves,)),
+            dma((2, leaves)), dma((2, leaves)), dma((2, leaves)), dma((2, leaves)), dma((leaves,)),
         ],
         compiler_params=pltpu.CompilerParams(collective_id=0, has_side_effects=True),
         name="whole",

time: 43.2 us -> 41.4 us (0.958)
  Pallas kernels: 40.4 us -> 38.6 us
    pallas_call x1, Pallas kernels: 40.4 us -> 38.6 us  [whole_call(): pl.pallas_call(functools.partial(whole_kernel, digits=digits, leaves=leav...]
where the time goes in v4:
time: 41.4 us; the launch traced here: 41.3 us
  Pallas kernels  38.6 us (93%)
  local copies, waits for them, and re-layouts  2.61 us (6%)
    pallas_call x1, Pallas kernels, whole_call(): pl.pallas_call(functools.partial(whole_kernel, digits=digits, leaves=leav...  38.6 us
    unnamed x1, local copies, waits for them, and re-layouts  2.61 us

profile of v4, /device:TPU:0, one launch (start us, length us, event | category | flops | bytes accessed | tf_op | source)
XLA Modules:
  0.0 41.3 jit_solution(15403363198423033041)
XLA Ops:
  0.0 38.6 %whole.1 = f32[4096,128]{1,0:T(8,128)} custom-call(s32[128,2,8,128]{3,2,1,0:T(8,128)} %bitcast.10, f32[2,128,2,8,128]{4,3,2,1,0:T(8,128)} %bitcast.9, bf16[2,512,512]{2,1,0:T(8,128)(2,1)} %constant.11.clone.w1_hbm, bf16[2,512,512]{2,1,0:T(8,128)(2,1)} %constant.12.clone.w2_hbm, bf16[2,256,256]{2,1,0:T(8,128)(2,1)} %constant.13.clone.w3_hbm, ...), custom_call_target="tpu_custom_call" | custom-call | tf_op jit(solution)/shard_map/whole/pallas_call | solution.py:728
  38.6 2.6 %copy.11 = f32[2,262144]{1,0:T(2,128)} copy(f32[2,262144]{1,0:T(2,128)} %bitcast.8) | data formatting | bytes 4194304

commit v5 on v4

--- a/solution.py
+++ b/solution.py
@@ -515,9 +515,11 @@
         for copy in take(g):
             copy.start()
     barrier = pltpu.get_barrier_semaphore()
+    signals = 0
     for d in range(leaves):
-        for peer in (blk_no, across) if d else (beside, across):
+        for peer in ([blk_no] if d else [beside]) + ([across] if d < leaves // 2 else []):
             pl.semaphore_signal(barrier, inc=1, device_id=(xor(me, d, bits), peer), device_id_type=mesh_id)
+            signals += 1
 
     cells_at = lax.broadcasted_iota(jnp.int32, (8, LANES), 1)
     cos_at, sin_at = cos_sin_turns((cells_at * (TOP_TICKS // 2)).astype(jnp.float32) * (2.0**-32))
@@ -547,6 +549,14 @@
                 result.append((u + x, w + z) if k == 0 else (u + cheb[k] * x, w + cheb[k] * z))
         return tuple(result)
 
+    def shuffle(g, d):
+        peer = xor(me, d, bits)
+        return pltpu.make_async_remote_copy(
+            src_ref=y.at[g, peer], dst_ref=got.at[g, me],
+            send_sem=send1.at[g, d], recv_sem=recv1.at[g, d],
+            device_id=(peer, blk_no), device_id_type=mesh_id,
+        )
+
     for g in range(groups):
         for copy in take(g):
             copy.wait()
@@ -570,29 +580,22 @@
             return carry
 
         lax.fori_loop(0, 8, tile, 0)
-
-    later[0].wait()
-    y[...] = mm3(w1, stack[...].reshape(digits * 2 * R, LANES)).reshape(y.shape)
-    pl.semaphore_wait(barrier, 2 * leaves)
-
-    def shuffle(d):
-        peer = xor(me, d, bits)
-        return pltpu.make_async_remote_copy(
-            src_ref=y.at[peer], dst_ref=got.at[me],
-            send_sem=send1.at[d - 1], recv_sem=recv1.at[d - 1],
-            device_id=(peer, blk_no), device_id_type=mesh_id,
-        )
-
-    for d in far_first(leaves):
-        shuffle(d).start()
-    got[me] = y[me]
-    for d in far_first(leaves):
-        shuffle(d).wait_recv()
-
-    n2, n3 = digits.bit_length() - 1, LANES.bit_length() - digits.bit_length()
+        if g == 0:
+            later[0].wait()
+            pl.semaphore_wait(barrier, signals)
+        y[g] = mm3(w1, stack[g * 8 : (g + 1) * 8].reshape(8 * 2 * R, LANES)).reshape(leaves, 2 * R, LANES)
+        for d in far_first(leaves):
+            shuffle(g, d).start()
+
+    got[:, me] = y[:, me]
+    for g in range(groups):
+        for d in range(1, leaves):
+            shuffle(g, d).wait_recv()
+
+    n2 = digits.bit_length() - 1
     for cg in range(2 * R // 8):
-        slots = [got[k, a * 2 * R + cg * 8 : a * 2 * R + cg * 8 + 8, :] for a in range(own) for k in range(leaves)]
-        slots = swap_bits(slots, [(k, k) for k in range(n2)])
+        slots = [got[j, k, cg * 8 : cg * 8 + 8, :] for k in range(leaves) for j in range(own)]
+        slots = swap_bits(slots, [(n2 - bits + k, k) for k in range(bits)])
         for k, v in enumerate(slots):
             x2[k * 2 * R + cg * 8 : k * 2 * R + cg * 8 + 8, :] = v
     later[1].wait()
@@ -600,20 +603,19 @@
     x2[...] = z2
     for cg in range(2 * R // 8):
         slots = [x2[k * 2 * R + cg * 8 : k * 2 * R + cg * 8 + 8, :] for k in range(digits)]
-        slots = swap_bits(slots, [(k, n3 + k) for k in range(n2)])
+        slots = swap_bits(slots, [(k, bits + k) for k in range(n2)])
         for k, v in enumerate(slots):
-            x3[k // own * 2 * R + cg * 8 : k // own * 2 * R + cg * 8 + 8, k % own * LANES : (k % own + 1) * LANES] = v
+            x3[k * 2 * R + cg * 8 : k * 2 * R + cg * 8 + 8, :] = v
     later[2].wait()
-    x4[...] = mm3(w3, x3[...])
+    z3 = mm3(w3, x3[...])
+    x3[...] = z3
     for cg in range(2 * R // 8):
-        for a in range(own):
-            cols = slice(a * LANES, (a + 1) * LANES)
-            slots = [x4[k * 2 * R + cg * 8 : k * 2 * R + cg * 8 + 8, cols] for k in range(leaves)]
-            slots = swap_bits(slots, [(k, k) for k in range(n3)])
-            for k, v in enumerate(slots):
-                x3[k * 2 * R + cg * 8 : k * 2 * R + cg * 8 + 8, cols] = v
+        slots = [x3[k * 2 * R + cg * 8 : k * 2 * R + cg * 8 + 8, :] for k in range(digits)]
+        slots = swap_bits(slots, [(n2 - bits + k, k) for k in range(bits)])
+        for k, v in enumerate(slots):
+            x4[k // own * 2 * R + cg * 8 : k // own * 2 * R + cg * 8 + 8, k % own * LANES : (k % own + 1) * LANES] = v
     later[3].wait()
-    z4 = mm3(w4, x3[...])
+    z4 = mm3(w4, x4[...])
     for a in range(own):
         mine[:, a] = z4[:, a * LANES : (a + 1) * LANES].reshape(leaves, 2 * R, LANES)
 
@@ -630,6 +632,13 @@
             device_id=(peer, across if way else blk_no), device_id_type=mesh_id,
         )
 
+    def relay(d):
+        here = coefs.at[blk_no, xor(me, d, bits)]
+        return pltpu.make_async_remote_copy(
+            src_ref=here, dst_ref=here, send_sem=send.at[1, d], recv_sem=recv.at[1, d],
+            device_id=(me, across), device_id_type=mesh_id,
+        )
+
     def forward(way, d):
         here = coefs.at[across if way else blk_no, xor(me, d, bits)]
         return pltpu.make_async_remote_copy(
@@ -644,7 +653,7 @@
     sin_poly = fit_even(lambda y: np.sin(2 * np.pi * y) / y, tilt, 3)
     cos_poly = [c * tilt ** (2 * k) for k, c in enumerate(cos_poly)]
     sin_poly = [c * tilt ** (2 * k + 1) for k, c in enumerate(sin_poly)]
-    below = lax.broadcasted_iota(jnp.int32, (rows, LANES), 0) * (leaves * ticks)
+    below = lax.broadcasted_iota(jnp.int32, (rows, LANES), 0) * (own * leaves * ticks)
 
     def tables(chunk, slot):
         parts = [split_pair(jnp.concatenate([coefs[q, chunk, t] for q in range(blocks)], axis=0).T) for t in range(own)]
@@ -658,8 +667,9 @@
     def points(chunk, slot):
         first = pl.multiple_of(chunk * width, width)
         for i in range(width // rows):
-            base = ((first + i * rows) * leaves + suffix) * ticks
-            u = (tgt[pl.ds(first + i * rows, rows), :] - (below + base)).astype(jnp.float32)
+            box = first + own * (i * rows % LANES) + i * rows // LANES
+            base = (box * leaves + suffix) * ticks
+            u = (tgt[pl.ds(box, rows, stride=own), :] - (below + base)).astype(jnp.float32)
             cell = (u * (1.0 / pitch) + (0.5 / pitch)).astype(jnp.int32)
             s = (u - cell.astype(jnp.float32) * pitch) * (2.0 / pitch) - 1.0
             got_at = [jnp.take_along_axis(tab[slot, n, i * rows : (i + 1) * rows, :], cell, axis=1)
@@ -671,44 +681,54 @@
             re = (re[0] + re[1]) + (re[2] + re[3]) + re[4]
             im = (im[0] + im[1]) + (im[2] + im[3]) + im[4]
             pc, ps = horner(cos_poly, z), s * horner(sin_poly, z)
-            out[pl.ds(2 * (first + i * rows), rows, stride=2), :] = pc * re - ps * im
-            out[pl.ds(2 * (first + i * rows) + 1, rows, stride=2), :] = pc * im + ps * re
+            out[pl.ds(2 * box, rows, stride=2 * own), :] = pc * re - ps * im
+            out[pl.ds(2 * box + 1, rows, stride=2 * own), :] = pc * im + ps * re
 
     def put(d):
         span = pl.ds(pl.multiple_of(xor(me, d, bits) * (2 * width), 2 * width), 2 * width)
         return pltpu.make_async_copy(out.at[span], out_hbm.at[span], osem.at[d])
 
-    order = [0] + far_first(leaves)
-    both = [(way, d) for d in order for way in range(2) if way or d]
-    for way, d in both:
-        ship(way, d).start()
+    order = list(range(leaves))
+    near = leaves // 2
+    for d in order:
+        for way in range(2 if d < near else 1):
+            if way or d:
+                ship(way, d).start()
     coefs[blk_no, me] = mine[suffix]
-    lag = 2
-    for step in range(leaves + lag + 1):
+    for step in range(leaves + 5):
         if step < leaves:
             d = order[step]
-            for way in range(2):
-                if way or d:
-                    ship(way, d).wait_recv()
-                forward(way, d).start()
-        if step == lag:
+            if d:
+                ship(0, d).wait_recv()
+            forward(0, d).start()
+            if d < near:
+                ship(1, d).wait_recv()
+                forward(1, d).start()
+            else:
+                relay(d).start()
+        if 0 <= step - 3 < leaves and order[step - 3] >= near:
+            d = order[step - 3]
+            relay(d).wait_recv()
+            forward(1, d).start()
+        if step == 4:
             later[4].wait()
             later[5].wait()
-        if 0 <= step - lag < leaves:
-            d = order[step - lag]
+        if 0 <= step - 4 < leaves:
+            d = order[step - 4]
             for way in range(2):
                 forward(way, d).wait_recv()
-            tables(xor(me, d, bits), (step - lag) % 2)
-        if 0 <= step - lag - 1:
-            d = order[step - lag - 1]
-            points(xor(me, d, bits), (step - lag - 1) % 2)
+            tables(xor(me, d, bits), step % 2)
+        if 0 <= step - 5:
+            d = order[step - 5]
+            points(xor(me, d, bits), (step - 1) % 2)
             put(d).start()
     for d in order:
         if d:
-            shuffle(d).wait_send()
+            for g in range(groups):
+                shuffle(g, d).wait_send()
+            ship(0, d).wait_send()
+        (ship(1, d) if d < near else relay(d)).wait_send()
         for way in range(2):
-            if way or d:
-                ship(way, d).wait_send()
             forward(way, d).wait_send()
         put(d).wait()
 
@@ -718,9 +738,8 @@
     digits = boxes // LANES
     groups = digits // 8
     own = digits // leaves
-    n1 = digits.bit_length() - 1
-    n3 = LANES.bit_length() - digits.bit_length()
-    n, m = digits * 2 * R, 2**n3 * 2 * R
+    n1, n2 = leaves.bit_length() - 1, digits.bit_length() - 1
+    n, m = digits * 2 * R, leaves * 2 * R
     grid = split_rows(grid_matrix(depth, blocks))
     anywhere = pl.BlockSpec(memory_space=pl.ANY)
     dma = pltpu.SemaphoreType.DMA
@@ -737,14 +756,14 @@
             pltpu.VMEM((2, LANES, LANES), f32),
             pltpu.VMEM((2, LANES, LANES), f32),
             pltpu.VMEM((digits, 2 * R, LANES), f32),
+            pltpu.VMEM((2, m, m), bf16),
             pltpu.VMEM((2, n, n), bf16),
             pltpu.VMEM((2, n, n), bf16),
             pltpu.VMEM((2, m, m), bf16),
-            pltpu.VMEM((2, m, m), bf16),
-            pltpu.VMEM((leaves, n // leaves, LANES), f32),
-            pltpu.VMEM((leaves, n // leaves, LANES), f32),
+            pltpu.VMEM((groups, leaves, 2 * R, LANES), f32),
+            pltpu.VMEM((groups, leaves, 2 * R, LANES), f32),
             pltpu.VMEM((n, LANES), f32),
-            pltpu.VMEM((m, own * LANES), f32),
+            pltpu.VMEM((n, LANES), f32),
             pltpu.VMEM((m, own * LANES), f32),
             pltpu.VMEM((leaves, own, 2 * R, LANES), f32),
             pltpu.VMEM((boxes, TGT_BOX), jnp.int32),
@@ -752,15 +771,15 @@
             pltpu.VMEM(grid.shape, bf16),
             pltpu.VMEM((2, 2 * (DEGREE + 1), own * LANES, LANES), f32),
             pltpu.VMEM((blocks, leaves, own, 2 * R, LANES), f32),
-            dma((3, groups)), dma((6,)), dma((leaves - 1,)), dma((leaves - 1,)),
+            dma((3, groups)), dma((6,)), dma((groups, leaves)), dma((groups, leaves)),
             dma((2, leaves)), dma((2, leaves)), dma((2, leaves)), dma((2, leaves)), dma((leaves,)),
         ],
         compiler_params=pltpu.CompilerParams(collective_id=0, has_side_effects=True),
         name="whole",
     )(
         pos.reshape(LANES, groups, 8, LANES), strengths.reshape(2, LANES, groups, 8, LANES),
-        two_parts(first_matrix(n1)), two_parts(radix_matrix(n1, n1)),
-        two_parts(radix_matrix(2 * n1, n3)), two_parts(radix_matrix(2 * n1 + n3, n3)),
+        two_parts(first_matrix(n1)), two_parts(radix_matrix(n1, n2)),
+        two_parts(radix_matrix(n1 + n2, n2)), two_parts(radix_matrix(n1 + 2 * n2, n1)),
         grid, ticks,
     )
 

time: 41.4 us -> 36.1 us (0.87)
  Pallas kernels: 38.6 us -> 33.4 us
    pallas_call x1, Pallas kernels: 38.6 us -> 33.4 us  [whole_call(): pl.pallas_call(functools.partial(whole_kernel, digits=digits, leaves=leav...]
where the time goes in v5:
time: 36.1 us; the launch traced here: 36 us
  Pallas kernels  33.4 us (93%)
  local copies, waits for them, and re-layouts  2.61 us (7%)
    pallas_call x1, Pallas kernels, whole_call(): pl.pallas_call(functools.partial(whole_kernel, digits=digits, leaves=leav...  33.4 us
    unnamed x1, local copies, waits for them, and re-layouts  2.61 us

profile of v5, /device:TPU:0, one launch (start us, length us, event | category | flops | bytes accessed | tf_op | source)
XLA Modules:
  0.0 36.0 jit_solution(12533957912832894624)
XLA Ops:
  0.0 33.4 %whole.1 = f32[4096,128]{1,0:T(8,128)} custom-call(s32[128,2,8,128]{3,2,1,0:T(8,128)} %bitcast.10, f32[2,128,2,8,128]{4,3,2,1,0:T(8,128)} %bitcast.9, bf16[2,256,256]{2,1,0:T(8,128)(2,1)} %constant.11.clone.w1_hbm, bf16[2,512,512]{2,1,0:T(8,128)(2,1)} %constant.12.clone.w2_hbm, bf16[2,512,512]{2,1,0:T(8,128)(2,1)} %constant.13.clone.w3_hbm, ...), custom_call_target="tpu_custom_call" | custom-call | tf_op jit(solution)/shard_map/whole/pallas_call | solution.py:747
  33.4 2.6 %copy.11 = f32[2,262144]{1,0:T(2,128)} copy(f32[2,262144]{1,0:T(2,128)} %bitcast.8) | data formatting | bytes 4194304

commit v6 on v5

--- a/solution.py
+++ b/solution.py
@@ -487,10 +487,10 @@
     return dot16(w[0], hi) + dot16(w[0], lo) + dot16(w[1], hi)
 
 
-def whole_kernel(pos_hbm, str_hbm, w1_hbm, w2_hbm, w3_hbm, w4_hbm, a_hbm, tgt_hbm, out_hbm,
+def whole_kernel(pos_hbm, str_hbm, w1_hbm, w2_hbm, w3_hbm, w4_hbm, a_hbm, tgt_hbm, out,
                  pos, amp, p_t, re_t, im_t, stack, w1, w2, w3, w4, y, got, x2, x3, x4, mine,
-                 tgt, out, a_buf, tab, coefs,
-                 isem, wsem, send1, recv1, send, recv, gsend, grecv, osem,
+                 tgt, a_buf, tab, coefs,
+                 isem, wsem, send1, recv1, send, recv, gsend, grecv,
                  *, digits, leaves, blocks, depth, rows):
     me, blk_no = lax.axis_index("leaf"), lax.axis_index("blk")
     bits = leaves.bit_length() - 1
@@ -683,10 +683,6 @@
             pc, ps = horner(cos_poly, z), s * horner(sin_poly, z)
             out[pl.ds(2 * box, rows, stride=2 * own), :] = pc * re - ps * im
             out[pl.ds(2 * box + 1, rows, stride=2 * own), :] = pc * im + ps * re
-
-    def put(d):
-        span = pl.ds(pl.multiple_of(xor(me, d, bits) * (2 * width), 2 * width), 2 * width)
-        return pltpu.make_async_copy(out.at[span], out_hbm.at[span], osem.at[d])
 
     order = list(range(leaves))
     near = leaves // 2
@@ -721,7 +717,6 @@
         if 0 <= step - 5:
             d = order[step - 5]
             points(xor(me, d, bits), (step - 1) % 2)
-            put(d).start()
     for d in order:
         if d:
             for g in range(groups):
@@ -730,7 +725,6 @@
         (ship(1, d) if d < near else relay(d)).wait_send()
         for way in range(2):
             forward(way, d).wait_send()
-        put(d).wait()
 
 
 def whole_call(pos, strengths, ticks, leaves, blocks, depth):
@@ -741,14 +735,14 @@
     n1, n2 = leaves.bit_length() - 1, digits.bit_length() - 1
     n, m = digits * 2 * R, leaves * 2 * R
     grid = split_rows(grid_matrix(depth, blocks))
-    anywhere = pl.BlockSpec(memory_space=pl.ANY)
+    anywhere = pl.BlockSpec(memory_space=pltpu.HBM)
     dma = pltpu.SemaphoreType.DMA
     f32, bf16 = jnp.float32, jnp.bfloat16
     return pl.pallas_call(
         functools.partial(whole_kernel, digits=digits, leaves=leaves, blocks=blocks, depth=depth, rows=8),
-        out_shape=jax.ShapeDtypeStruct((2 * boxes, TGT_BOX), f32),
+        out_shape=pltpu.VMEM((2 * boxes, TGT_BOX), f32),
         in_specs=[anywhere] * 8,
-        out_specs=anywhere,
+        out_specs=pl.BlockSpec(memory_space=pltpu.VMEM),
         scratch_shapes=[
             pltpu.VMEM((groups, LANES, 8, LANES), jnp.int32),
             pltpu.VMEM((2, groups, LANES, 8, LANES), f32),
@@ -767,14 +761,13 @@
             pltpu.VMEM((m, own * LANES), f32),
             pltpu.VMEM((leaves, own, 2 * R, LANES), f32),
             pltpu.VMEM((boxes, TGT_BOX), jnp.int32),
-            pltpu.VMEM((2 * boxes, TGT_BOX), f32),
             pltpu.VMEM(grid.shape, bf16),
             pltpu.VMEM((2, 2 * (DEGREE + 1), own * LANES, LANES), f32),
             pltpu.VMEM((blocks, leaves, own, 2 * R, LANES), f32),
             dma((3, groups)), dma((6,)), dma((groups, leaves)), dma((groups, leaves)),
-            dma((2, leaves)), dma((2, leaves)), dma((2, leaves)), dma((2, leaves)), dma((leaves,)),
+            dma((2, leaves)), dma((2, leaves)), dma((2, leaves)), dma((2, leaves)),
         ],
-        compiler_params=pltpu.CompilerParams(collective_id=0, has_side_effects=True),
+        compiler_params=pltpu.CompilerParams(collective_id=0, has_side_effects=True, vmem_limit_bytes=60 * 10**6),
         name="whole",
     )(
         pos.reshape(LANES, groups, 8, LANES), strengths.reshape(2, LANES, groups, 8, LANES),
@@ -784,11 +777,35 @@
     )
 
 
+def hand_over(x_ref, out_hbm, sem):
+    parts = sem.shape[0]
+    size = x_ref.shape[0] // parts
+    copies = [pltpu.make_async_copy(x_ref.at[pl.ds(k * size, size)], out_hbm.at[pl.ds(k * size, size)], sem.at[k])
+              for k in range(parts)]
+    for copy in copies:
+        copy.start()
+    for copy in copies:
+        copy.wait()
+
+
+def hand_over_call(x):
+    return pl.pallas_call(
+        hand_over,
+        out_shape=jax.ShapeDtypeStruct(x.shape, x.dtype),
+        in_specs=[pl.BlockSpec(memory_space=pltpu.VMEM)],
+        out_specs=pl.BlockSpec(memory_space=pl.ANY),
+        scratch_shapes=[pltpu.SemaphoreType.DMA((8,))],
+        compiler_params=pltpu.CompilerParams(vmem_limit_bytes=16 * 2**20),
+        name="hand_over",
+    )(x)
+
+
 def local_two_shuffles(src_pos, strengths, tgt_pos):
     leaves, blocks = lax.axis_size("leaf"), lax.axis_size("blk")
     boxes = src_pos.shape[1] // PER_BOX
     depth = boxes.bit_length() - 1 + leaves.bit_length() - 1
     out = whole_call(src_pos, strengths, tgt_pos.reshape(boxes, TGT_BOX), leaves, blocks, depth)
+    out = hand_over_call(out)
     return out.reshape(boxes, 2, TGT_BOX).transpose(1, 0, 2).reshape(2, boxes * TGT_BOX)
 
 

time: 36.1 us -> 34.2 us (0.947)
  local copies, waits for them, and re-layouts: 2.61 us -> 0 us
  Pallas kernels: 33.4 us -> 34 us
    unnamed x1 -> x0, local copies, waits for them, and re-layouts: 2.61 us -> none
    pallas_call x0 -> x1, Pallas kernels: none -> 1.38 us  [hand_over_call(): pl.pallas_call(hand_over, out_shape=jax.ShapeDtypeStruct(x.shape, x.dtype...]
    pallas_call x1, Pallas kernels: 33.4 us -> 32.7 us  [whole_call(): pl.pallas_call(functools.partial(whole_kernel, digits=digits, leaves=leav...]
where the time goes in v6:
time: 34.2 us; the launch traced here: 34 us
  Pallas kernels  34 us (99%)
    pallas_call x1, Pallas kernels, whole_call(): pl.pallas_call(functools.partial(whole_kernel, digits=digits, leaves=leav...  32.7 us
    pallas_call x1, Pallas kernels, hand_over_call(): pl.pallas_call(hand_over, out_shape=jax.ShapeDtypeStruct(x.shape, x.dtype...  1.38 us

profile of v6, /device:TPU:0, one launch (start us, length us, event | category | flops | bytes accessed | tf_op | source)
XLA Modules:
  0.0 34.0 jit_solution(4660951215780849150)
XLA Ops:
  0.0 32.7 %whole.1.x_ref = f32[4096,128]{1,0:T(8,128)S(1)} custom-call(s32[128,2,8,128]{3,2,1,0:T(8,128)} %bitcast.9, f32[2,128,2,8,128]{4,3,2,1,0:T(8,128)} %bitcast.8, bf16[2,256,256]{2,1,0:T(8,128)(2,1)} %constant.11.clone.w1_hbm, bf16[2,512,512]{2,1,0:T(8,128)(2,1)} %constant.12.clone.w2_hbm, bf16[2,512,512]{2,1,0:T(8,128)(2,1)} %constant.13.clone.w3_hbm, ...), custom_call_target="tpu_custom_call" | custom-call | tf_op jit(solution)/shard_map/whole/pallas_call | solution.py:741
  32.7 1.4 %hand_over.1 = f32[4096,128]{1,0:T(8,128)} custom-call(f32[4096,128]{1,0:T(8,128)S(1)} %whole.1.x_ref), custom_call_target="tpu_custom_call" | custom-call | tf_op jit(solution)/shard_map/hand_over/pallas_call | solution.py:792

commit v7 on v6

--- a/solution.py
+++ b/solution.py
@@ -511,9 +511,8 @@
         pltpu.make_async_copy(src, dst, wsem.at[k])
         for k, (src, dst) in enumerate([(w1_hbm, w1), (w2_hbm, w2), (w3_hbm, w3), (w4_hbm, w4), (a_hbm, a_buf), (tgt_hbm, tgt)])
     ]
-    for g in range(groups):
-        for copy in take(g):
-            copy.start()
+    for copy in take(0):
+        copy.start()
     barrier = pltpu.get_barrier_semaphore()
     signals = 0
     for d in range(leaves):
@@ -561,7 +560,7 @@
         for copy in take(g):
             copy.wait()
         if g == 0:
-            for copy in later:
+            for copy in [copy for h in range(1, groups) for copy in take(h)] + later:
                 copy.start()
         turn_over(g, 0, 0)
 
@@ -587,19 +586,24 @@
         for d in far_first(leaves):
             shuffle(g, d).start()
 
-    got[:, me] = y[:, me]
-    for g in range(groups):
+    n2 = digits.bit_length() - 1
+    for j in range(own):
+        got[j, me] = y[j, me]
         for d in range(1, leaves):
-            shuffle(g, d).wait_recv()
-
-    n2 = digits.bit_length() - 1
-    for cg in range(2 * R // 8):
-        slots = [got[j, k, cg * 8 : cg * 8 + 8, :] for k in range(leaves) for j in range(own)]
-        slots = swap_bits(slots, [(n2 - bits + k, k) for k in range(bits)])
-        for k, v in enumerate(slots):
-            x2[k * 2 * R + cg * 8 : k * 2 * R + cg * 8 + 8, :] = v
-    later[1].wait()
-    z2 = mm3(w2, x2[...])
+            shuffle(j, d).wait_recv()
+        for cg in range(2 * R // 8):
+            slots = [got[j, k, cg * 8 : cg * 8 + 8, :] for k in range(leaves)]
+            slots = swap_bits(slots, [(k, k) for k in range(bits)])
+            for k, v in enumerate(slots):
+                first = (j * leaves + k) * 2 * R + cg * 8
+                x2[first : first + 8, :] = v
+        if j == 0:
+            later[1].wait()
+        span = slice(j * leaves * 2 * R, (j + 1) * leaves * 2 * R)
+        term = mm3((w2[0, :, span], w2[1, :, span]), x2[span, :])
+        if j < own - 1:
+            x3[...] = term if j == 0 else x3[...] + term
+    z2 = x3[...] + term
     x2[...] = z2
     for cg in range(2 * R // 8):
         slots = [x2[k * 2 * R + cg * 8 : k * 2 * R + cg * 8 + 8, :] for k in range(digits)]
@@ -691,7 +695,7 @@
             if way or d:
                 ship(way, d).start()
     coefs[blk_no, me] = mine[suffix]
-    for step in range(leaves + 5):
+    for step in range(leaves + 6):
         if step < leaves:
             d = order[step]
             if d:
@@ -702,20 +706,20 @@
                 forward(1, d).start()
             else:
                 relay(d).start()
-        if 0 <= step - 3 < leaves and order[step - 3] >= near:
-            d = order[step - 3]
+        if 0 <= step - 4 < leaves and order[step - 4] >= near:
+            d = order[step - 4]
             relay(d).wait_recv()
             forward(1, d).start()
-        if step == 4:
+        if step == 5:
             later[4].wait()
             later[5].wait()
-        if 0 <= step - 4 < leaves:
-            d = order[step - 4]
+        if 0 <= step - 5 < leaves:
+            d = order[step - 5]
             for way in range(2):
                 forward(way, d).wait_recv()
             tables(xor(me, d, bits), step % 2)
-        if 0 <= step - 5:
-            d = order[step - 5]
+        if 0 <= step - 6:
+            d = order[step - 6]
             points(xor(me, d, bits), (step - 1) % 2)
     for d in order:
         if d:
@@ -725,6 +729,11 @@
         (ship(1, d) if d < near else relay(d)).wait_send()
         for way in range(2):
             forward(way, d).wait_send()
+
+
+def halves_first(m, own):
+    rows = m.shape[0]
+    return m.reshape(rows, -1, own, 2 * R).transpose(0, 2, 1, 3).reshape(rows, -1)
 
 
 def whole_call(pos, strengths, ticks, leaves, blocks, depth):
@@ -771,7 +780,7 @@
         name="whole",
     )(
         pos.reshape(LANES, groups, 8, LANES), strengths.reshape(2, LANES, groups, 8, LANES),
-        two_parts(first_matrix(n1)), two_parts(radix_matrix(n1, n2)),
+        two_parts(first_matrix(n1)), two_parts(halves_first(radix_matrix(n1, n2), own)),
         two_parts(radix_matrix(n1 + n2, n2)), two_parts(radix_matrix(n1 + 2 * n2, n1)),
         grid, ticks,
     )

time: 34.2 us -> 33.6 us (0.982)
  Pallas kernels: 34 us -> 33.4 us
    pallas_call x1, Pallas kernels: 32.7 us -> 32 us  [whole_call(): pl.pallas_call(functools.partial(whole_kernel, digits=digits, leaves=leav...]
where the time goes in v7:
time: 33.6 us; the launch traced here: 33.4 us
  Pallas kernels  33.4 us (99%)
    pallas_call x1, Pallas kernels, whole_call(): pl.pallas_call(functools.partial(whole_kernel, digits=digits, leaves=leav...  32 us
    pallas_call x1, Pallas kernels, hand_over_call(): pl.pallas_call(hand_over, out_shape=jax.ShapeDtypeStruct(x.shape, x.dtype...  1.38 us

profile of v7, /device:TPU:0, one launch (start us, length us, event | category | flops | bytes accessed | tf_op | source)
XLA Modules:
  0.0 33.4 jit_solution(2876877343177635479)
XLA Ops:
  0.0 32.0 %whole.1.x_ref = f32[4096,128]{1,0:T(8,128)S(1)} custom-call(s32[128,2,8,128]{3,2,1,0:T(8,128)} %bitcast.9, f32[2,128,2,8,128]{4,3,2,1,0:T(8,128)} %bitcast.8, bf16[2,256,256]{2,1,0:T(8,128)(2,1)} %constant.11.clone.w1_hbm, bf16[2,512,512]{2,1,0:T(8,128)(2,1)} %constant.12.clone.w2_hbm, bf16[2,512,512]{2,1,0:T(8,128)(2,1)} %constant.13.clone.w3_hbm, ...), custom_call_target="tpu_custom_call" | custom-call | tf_op jit(solution)/shard_map/whole/pallas_call | solution.py:750
  32.0 1.4 %hand_over.1 = f32[4096,128]{1,0:T(8,128)} custom-call(f32[4096,128]{1,0:T(8,128)S(1)} %whole.1.x_ref), custom_call_target="tpu_custom_call" | custom-call | tf_op jit(solution)/shard_map/hand_over/pallas_call | solution.py:801
